TPU v7x, 32 devices: a whole 2x2x4 slice. The times are simulated.
32 devices in a mesh: gx: 2 (over y), gy: 4 (over x, core), gz: 4 (over z).
Axes of the slice: x: 2, y: 2, z: 4, core: 2. Of those that a mesh axis runs over, the one named last changes fastest.
Arguments:
- log_range: float32 [64, 128, 512], P('gx', 'gy', 'gz'), may hold values from 0.7 to 2
- state: float32 [2, 64, 128, 512], P(None, 'gx', 'gy', 'gz'), may hold values from -60 to 60, as said below
- adjoint_start: float32 [2, 64, 128, 512], P(None, 'gx', 'gy', 'gz'), may hold values from -0.3 to 0.3
- obs_index: int32 [2, 2, 4, 4, 4096], P(None, 'gx', 'gy', 'gz'), may hold values from 0 to 131071
- obs_value: float32 [2, 2, 4, 4, 4096], P(None, 'gx', 'gy', 'gz'), may hold values from -6 to 6
Outputs:
- gradient: float32 [64, 128, 512], P('gx', 'gy', 'gz')
- adjoint: float32 [2, 64, 128, 512], P(None, 'gx', 'gy', 'gz')
Inputs may be any that keep to these rules, and one draw needn't show every extreme that they name: `obs_index`: each entry numbers a cell of its own device's block as (a * 32 + b) * 128 + c; cells may repeat. `state`: real values.
All inputs are finite; a program needn't handle non-finite values.
Results may differ from a plain program's by a relative error of at most 0.0001.
Values sent between devices are 32-bit elements; how exact they have to be, the bound alone decides.
A program may use at most 320 MiB of HBM per device.

v0:
```python
import functools
import itertools

import jax
import jax.numpy as jnp
from jax import lax
from jax.experimental import pallas as pl
from jax.experimental.pallas import tpu as pltpu
from jax.sharding import PartitionSpec as P

ITERS = 4
LANES = 128
AXES = ("gx", "gy", "gz")
MESH = pl.DeviceIdType.MESH

noise_var = 0.25


def kernel(
    sizes, dims, lr_ref, state_ref, start_ref, idx_ref, val_ref, grad_ref, adj_ref,
    ext, ysend, yrecv, zsend, zrecv, zboth, kap, weight, values, rhs_hot, res, image,
    xi, ast, res_image, d, di, s_buf, z_buf, q_buf, red_out, red, send_sem, recv_sem, red_send, red_recv,
):
    sets, cx, cy, cz, nobs = dims
    rows = cx * cy
    place = [lax.axis_index(axis) for axis in AXES]
    rank = (place[0] * sizes[1] + place[1]) * sizes[2] + place[2]
    total = sizes[0] * sizes[1] * sizes[2]
    lane = lax.broadcasted_iota(jnp.int32, (cy, LANES), 1)
    row = lax.broadcasted_iota(jnp.int32, (cy, LANES), 0)
    pair = lane // 2
    even = lane % 2 == 0
    small_lane = lax.broadcasted_iota(jnp.int32, (1, LANES), 1)
    offsets = [o for o in itertools.product(*[range(n) for n in sizes]) if any(o)]

    def device_at(offset):
        return tuple(lax.rem(p + o, n) for p, o, n in zip(place, offset, sizes))

    barrier = pltpu.get_barrier_semaphore()
    for offset in offsets:
        pl.semaphore_signal(barrier, inc=1, device_id=device_at(offset), device_id_type=MESH)

    def inner(x):
        return pl.ds(pl.multiple_of((x + 1) * cy, cy), cy)

    def plain(x):
        return pl.ds(pl.multiple_of(x * cy, cy), cy)

    def fold(v):
        return jnp.sum(v.reshape(cy // 8, 8, LANES), axis=0)

    def sweep(body, slot=None, sums=0):
        zero = jnp.zeros((cy, LANES), jnp.float32)
        faces = (zero,) * sets if slot is not None else ()

        def step(x, carry):
            faces, gathered = carry
            packed, added = [], []
            for s in range(sets):
                slab, terms = body(s, x)
                if slot is not None:
                    at = s * cx + x
                    packed.append(jnp.where(pair == at, pltpu.roll(slab, 2 * at + 1, 1), faces[s]))
                added.append(tuple(a + fold(t) for a, t in zip(gathered[s], terms)))
            return tuple(packed), tuple(added)

        start = tuple(tuple(jnp.zeros((8, LANES), jnp.float32) for _ in range(sums)) for _ in range(sets))
        faces, gathered = lax.fori_loop(0, cx, step, (faces, start), unroll=8)
        if slot is not None:
            zsend[slot] = functools.reduce(jnp.add, faces)
            for s in range(sets):
                ysend[slot, 0, s * cx:(s + 1) * cx] = ext[slot, s, pl.ds(cy, cx, stride=cy), :]
                ysend[slot, 1, s * cx:(s + 1) * cx] = ext[slot, s, pl.ds(2 * cy - 1, cx, stride=cy), :]
        return gathered

    def copies(slot):
        near = [[tuple(sign if i == axis else 0 for i in range(3)) for sign in (-1, 1)] for axis in range(3)]
        ends = [
            (ext.at[slot, :, pl.ds(cy, cy), :], ext.at[slot, :, pl.ds((cx + 1) * cy, cy), :]),
            (ext.at[slot, :, pl.ds(cx * cy, cy), :], ext.at[slot, :, pl.ds(0, cy), :]),
            (ysend.at[slot, 0], yrecv.at[slot, 1]),
            (ysend.at[slot, 1], yrecv.at[slot, 0]),
            (zsend.at[slot], zrecv.at[slot, 1]),
            (zsend.at[slot], zrecv.at[slot, 0]),
        ]
        out = []
        for n, (src, dst) in enumerate(ends):
            offset = tuple(o % size for o, size in zip(near[n // 2][n % 2], sizes))
            out.append(pltpu.make_async_remote_copy(
                src_ref=src, dst_ref=dst, send_sem=send_sem.at[slot, n], recv_sem=recv_sem.at[slot, n],
                device_id=device_at(offset), device_id_type=MESH))
        return out

    def send(slot):
        for copy in copies(slot):
            copy.start()

    def arrive(slot):
        for copy in copies(slot):
            copy.wait()
        zboth[slot] = jnp.where(even, zrecv[slot, 0], pltpu.roll(zrecv[slot, 1], LANES - 2, 1))

    def apply(slot, s, x):
        center = ext[slot, s, inner(x), :]
        beside = ext[slot, s, inner(x + 1), :] + ext[slot, s, inner(x - 1), :]
        before = yrecv[slot, 0, pl.ds(s * cx + x, 1), :]
        after = yrecv[slot, 1, pl.ds(s * cx + x, 1), :]
        base = (x + 1) * cy
        beside = beside + jnp.where(row == cy - 1, after, pltpu.roll(center, cy - 1, 0))
        beside = beside + jnp.where(row == 0, before, pltpu.roll(center, 1, 0))
        edge = pltpu.roll(zboth[slot], lax.rem(LANES - 2 * (s * cx + x), LANES), 1)
        beside = beside + jnp.where(lane == LANES - 1, edge, pltpu.roll(center, LANES - 1, 1))
        beside = beside + jnp.where(lane == 0, edge, pltpu.roll(center, 1, 1))
        return (kap[plain(x), :] + 6.0) * center - beside

    def reduce_start(n, gathered):
        line = jnp.zeros((1, LANES), jnp.float32)
        for s in range(sets):
            for j in range(2):
                value = jnp.sum(jnp.sum(gathered[s][j], axis=0, keepdims=True), axis=1, keepdims=True)
                line = jnp.where(small_lane == 2 * s + j, value, line)
        red_out[n] = line
        red[n, rank] = line
        for offset in offsets:
            pltpu.make_async_remote_copy(
                src_ref=red_out.at[n], dst_ref=red.at[n, rank], send_sem=red_send.at[n],
                recv_sem=red_recv.at[n], device_id=device_at(offset), device_id_type=MESH).start()

    def reduce_end(n):
        many = red.at[n, pl.ds(0, total - 1)]
        pltpu.make_async_copy(many, many, red_recv.at[n]).wait()
        pltpu.make_async_copy(many, many, red_send.at[n]).wait()
        line = jnp.sum(red[n], axis=0)
        def pick(j):
            value = jnp.sum(jnp.where(small_lane == j, line, 0.0), axis=1, keepdims=True)
            return jnp.broadcast_to(value, (1, LANES))
        return [(pick(2 * s), pick(2 * s + 1)) for s in range(sets)]

    def load(slot, ref):
        def body(s, x):
            slab = ref[s, plain(x), :]
            ext[slot, s, inner(x), :] = slab
            return slab, ()
        sweep(body, slot)

    load(0, start_ref)
    load(2, state_ref)
    pl.semaphore_wait(barrier, total - 1)
    send(0)
    send(2)

    kap[...] = 4.0 * jnp.exp(-2.0 * lr_ref[...])

    tile = min(rows, 256)
    hot_lane = lax.broadcasted_iota(jnp.int32, (LANES, nobs), 0)
    for s in range(sets):
        cell = idx_ref[s:s + 1, :]
        value = val_ref[s:s + 1, :]
        hit = hot_lane == cell % cz
        top = value.astype(jnp.bfloat16).astype(jnp.float32)
        rhs_hot[0:LANES] = jnp.where(hit, 1.0, 0.0).astype(jnp.bfloat16)
        rhs_hot[LANES:2 * LANES] = jnp.where(hit, top, 0.0).astype(jnp.bfloat16)
        rhs_hot[2 * LANES:] = jnp.where(hit, value - top, 0.0).astype(jnp.bfloat16)
        line = cell // cz

        def step(m, carry, s=s, line=line):
            base = m * tile
            ids = lax.broadcasted_iota(jnp.int32, (tile, nobs), 0) + base
            hot = jnp.where(ids == line, 1.0, 0.0).astype(jnp.bfloat16)
            got = lax.dot_general(hot, rhs_hot[...], (((1,), (1,)), ((), ())), preferred_element_type=jnp.float32)
            at = pl.ds(pl.multiple_of(base, tile), tile)
            weight[s, at, :] = got[:, :LANES] * (1.0 / noise_var)
            values[s, at, :] = (got[:, LANES:2 * LANES] + got[:, 2 * LANES:]) * (1.0 / noise_var)
            return carry
        lax.fori_loop(0, rows // tile, step, 0)

    def start_pass(s, x):
        out = apply(0, s, x)
        ext[1, s, inner(x), :] = out
        xi[s, plain(x), :] = out
        return out, ()

    arrive(0)
    sweep(start_pass, 1)
    send(1)

    def right_pass(s, x):
        at = plain(x)
        right = values[s, at, :] - weight[s, at, :] * (state_ref[s, at, :] + start_ref[s, at, :])
        res[s, at, :] = right
        return right, ()

    sweep(right_pass)
    arrive(1)

    def residual_pass(s, x):
        out = res[s, plain(x), :] - apply(1, s, x)
        res[s, plain(x), :] = out
        ext[0, s, inner(x), :] = out
        return out, ()

    sweep(residual_pass, 0)
    send(0)

    def state_pass(s, x):
        out = apply(2, s, x)
        ast[s, plain(x), :] = out
        return out, ()

    arrive(2)
    sweep(state_pass)
    arrive(0)

    def inner_pass(s, x):
        out = apply(0, s, x)
        ext[1, s, inner(x), :] = out
        res_image[s, plain(x), :] = out
        return out, ()

    sweep(inner_pass, 1)
    send(1)
    arrive(1)

    def image_pass(s, x):
        now = res[s, plain(x), :]
        out = apply(1, s, x) + weight[s, plain(x), :] * now
        ext[0, s, inner(x), :] = out
        return out, (now * now, now * out)

    gathered = sweep(image_pass, 0, 2)
    send(0)
    reduce_start(0, gathered)

    def next_inner(s, x):
        out = apply(0, s, x)
        ext[1, s, inner(x), :] = out
        return out, ()

    def next_image(s, x):
        out = apply(1, s, x) + weight[s, plain(x), :] * ext[0, s, inner(x), :]
        image[s, plain(x), :] = out
        return out, ()

    norms = steps = None
    for k in range(ITERS):
        last = k + 1 == ITERS
        if not last:
            arrive(0)
            sweep(next_inner, 1)
            send(1)
            arrive(1)
            sweep(next_image)
        sums = reduce_end(k)
        if k == 0:
            ratio = None
            step_size = [norm / product for norm, product in sums]
        else:
            ratio = [sums[s][0] / norms[s] for s in range(sets)]
            step_size = [sums[s][0] / (sums[s][1] - ratio[s] * sums[s][0] / steps[s]) for s in range(sets)]
        norms, steps = [norm for norm, product in sums], step_size

        def follow(buf, s, at, new, ratio=ratio):
            if ratio is not None:
                new = new + ratio[s] * buf[s, at, :]
            return new

        if last:
            def finish(x, carry):
                at = plain(x)
                grad = jnp.zeros((cy, LANES), jnp.float32)
                for s in range(sets):
                    adj = adj_ref[s, at, :] + step_size[s] * follow(d, s, at, res[s, at, :])
                    adj_ref[s, at, :] = adj
                    applied = xi[s, at, :] + step_size[s] * follow(di, s, at, res_image[s, at, :])
                    grad = grad + (adj * ast[s, at, :] + applied * state_ref[s, at, :])
                grad_ref[at, :] = -2.0 * kap[at, :] * grad
                return carry
            lax.fori_loop(0, cx, finish, 0, unroll=8)
            break

        def update(s, x):
            at = plain(x)
            now, vec = res[s, at, :], ext[0, s, inner(x), :]
            z_new = follow(z_buf, s, at, image[s, at, :])
            s_new = follow(s_buf, s, at, vec)
            d[s, at, :] = follow(d, s, at, now)
            z_buf[s, at, :] = z_new
            s_buf[s, at, :] = s_new
            vec = vec - step_size[s] * z_new
            now = now - step_size[s] * s_new
            ext[0, s, inner(x), :] = vec
            res[s, at, :] = now
            return vec, (now * now, now * vec)

        more = k + 2 < ITERS
        gathered = sweep(update, 0 if more else None, 2)
        if more:
            send(0)
        reduce_start(k + 1, gathered)

        def trail(s, x):
            at = plain(x)
            base = start_ref if k == 0 else adj_ref
            adj_ref[s, at, :] = base[s, at, :] + step_size[s] * d[s, at, :]
            di_new = follow(di, s, at, res_image[s, at, :])
            di[s, at, :] = di_new
            xi[s, at, :] = xi[s, at, :] + step_size[s] * di_new
            q_new = follow(q_buf, s, at, ext[1, s, inner(x), :])
            q_buf[s, at, :] = q_new
            res_image[s, at, :] = res_image[s, at, :] - step_size[s] * q_new
            return q_new, ()

        sweep(trail)


def on_device(sizes, log_range, state, adjoint_start, obs_index, obs_value):
    sets, cx, cy, cz = state.shape
    nobs = obs_index.shape[-1]
    rows = cx * cy
    total = sizes[0] * sizes[1] * sizes[2]
    field = pltpu.VMEM((sets, rows, cz), jnp.float32)
    vmem = pl.BlockSpec(memory_space=pltpu.VMEM)
    gradient, adjoint = pl.pallas_call(
        functools.partial(kernel, sizes, (sets, cx, cy, cz, nobs)),
        out_shape=(
            jax.ShapeDtypeStruct((rows, cz), jnp.float32),
            jax.ShapeDtypeStruct((sets, rows, cz), jnp.float32),
        ),
        in_specs=[vmem] * 5,
        out_specs=(vmem, vmem),
        scratch_shapes=[
            pltpu.VMEM((3, sets, rows + 2 * cy, cz), jnp.float32),
            pltpu.VMEM((3, 2, sets * cx, cz), jnp.float32),
            pltpu.VMEM((3, 2, sets * cx, cz), jnp.float32),
            pltpu.VMEM((3, cy, LANES), jnp.float32),
            pltpu.VMEM((3, 2, cy, LANES), jnp.float32),
            pltpu.VMEM((3, cy, LANES), jnp.float32),
            pltpu.VMEM((rows, cz), jnp.float32),
            field,
            field,
            pltpu.VMEM((3 * LANES, nobs), jnp.bfloat16),
            *([field] * 10),
            pltpu.VMEM((ITERS, 1, LANES), jnp.float32),
            pltpu.VMEM((ITERS, total, 1, LANES), jnp.float32),
            pltpu.SemaphoreType.DMA((3, 6)),
            pltpu.SemaphoreType.DMA((3, 6)),
            pltpu.SemaphoreType.DMA((ITERS,)),
            pltpu.SemaphoreType.DMA((ITERS,)),
        ],
        compiler_params=pltpu.CompilerParams(
            collective_id=0, has_side_effects=True, vmem_limit_bytes=60 * 1024 * 1024
        ),
    )(
        log_range.reshape(rows, cz),
        state.reshape(sets, rows, cz),
        adjoint_start.reshape(sets, rows, cz),
        obs_index.reshape(sets, nobs),
        obs_value.reshape(sets, nobs),
    )
    return gradient.reshape(cx, cy, cz), adjoint.reshape(sets, cx, cy, cz)


def solution(mesh):
    in_specs = (
        P("gx", "gy", "gz"),
        P(None, "gx", "gy", "gz"),
        P(None, "gx", "gy", "gz"),
        P(None, "gx", "gy", "gz", None),
        P(None, "gx", "gy", "gz", None),
    )
    out_specs = (P("gx", "gy", "gz"), P(None, "gx", "gy", "gz"))
    sizes = tuple(mesh.shape[axis] for axis in AXES)
    return jax.shard_map(
        functools.partial(on_device, sizes), mesh=mesh, in_specs=in_specs, out_specs=out_specs, check_vma=False
    )
```

profile of v0, /device:TPU:0, one launch (start us, length us, event | category | flops | bytes accessed | tf_op | source)
XLA Modules:
  0.0 95.8 jit_solution(10787843115729625813)
XLA Ops:
  0.6 0.0 copy-start.1
  0.6 1.4 %copy.12 = s32[2,1,1,1,4096]{4,0,2,1,3:T(2,128)} copy(s32[2,1,1,1,4096]{4,3,2,1,0:T(1,128)} %param.8) | data formatting | bytes 65536
  2.0 0.0 copy-done.1
  2.0 0.6 copy.11
  2.7 90.1 %shard_map.68 = (f32[1024,128]{1,0:T(8,128)}, f32[2,1024,128]{2,1,0:T(8,128)}) custom-call(f32[1024,128]{1,0:T(8,128)} %bitcast.15, f32[2,1024,128]{2,1,0:T(8,128)} %bitcast.12, f32[2,1024,128]{2,1,0:T(8,128)} %bitcast.13, s32[2,4096]{1,0:T(2,128)} %bitcast.16, f32[2,4096]{1,0:T(2,128)} %bitcast.17), custom_call_target="tpu_custom_call" | custom-call | tf_op jit(solution)/shard_map/pallas_call | solution.py:323
  92.8 0.0 copy-start
  92.8 2.0 %copy.15 = f32[32,32,128]{2,1,0:T(8,128)} copy(f32[32,32,128]{2,1,0:T(8,128)} %bitcast.14) | data formatting | bytes 1048576
  94.8 0.0 copy-done
  94.8 1.0 %copy.16 = f32[2,32,32,128]{3,2,1,0:T(8,128)} copy(f32[2,32,32,128]{3,2,1,0:T(8,128)S(1)} %bitcast.11) | data formatting | bytes 2097152
Async XLA Ops:
  0.6 1.4 %copy-start.1 = (f32[2,1,1,1,4096]{4,3,2,1,0:T(1,128)S(1)}, f32[2,1,1,1,4096]{4,3,2,1,0:T(1,128)}, u32[]{:S(2)}) copy-start(f32[2,1,1,1,4096]{4,3,2,1,0:T(1,128)} %param.9) | copy-start | bytes 98308
  92.8 2.0 %copy-start = (f32[2,1024,128]{2,1,0:T(8,128)S(1)}, f32[2,1024,128]{2,1,0:T(8,128)}, u32[]{:S(2)}) copy-start(f32[2,1024,128]{2,1,0:T(8,128)} %get-tuple-element.5) | copy-start | bytes 3145732
where the time goes:
time: 96 us; the launch traced here: 95.8 us
  Pallas kernels  90.1 us (94%)
  local copies, waits for them, and re-layouts  4.98 us (5%)
    pallas_call x1, Pallas kernels, on_device(): pl.pallas_call(functools.partial(kernel, sizes, (sets, cx, cy, cz, nobs))...  90.1 us
    unnamed x8, local copies, waits for them, and re-layouts  4.98 us

commit v1 on v0

v1 whole, which is shorter than its diff:
```python
import functools
import itertools

import jax
import jax.numpy as jnp
from jax import lax
from jax.experimental import pallas as pl
from jax.experimental.pallas import tpu as pltpu
from jax.sharding import PartitionSpec as P

ITERS = 4
LANES = 128
HALF = LANES // 2
GHOST = 2
PAD = 8
AXES = ("gx", "gy", "gz")
MESH = pl.DeviceIdType.MESH
UNROLL = 8
X0, R0, W0, W1, W2, STATE, KAP, FIELDS = range(8)
DEEP = (X0, R0, W0, W1)
COPIES = 24

noise_var = 0.25


def kernel(
    sizes, dims, lr_ref, state_ref, start_ref, idx_ref, val_ref, grad_ref, adj_ref,
    ext, uext, ysend, yrecv, zsend, zrecv, zown, xysend, xyrecv, xzsend, xzrecv,
    ck, cp, xe, uz, kz, kap, hot, cols, raw, weight, rhs, z, s_buf, r, ar, q, ast, d, ad, xs, axs,
    xn, rn, dn, gx, gr, gd, red_out, red, send_sem, recv_sem, red_send, red_recv,
):
    sets, cx, cy, cz, nobs = dims
    pitch = cy + PAD
    slabs = cx + 2 * GHOST
    block = slabs * pitch
    lines = cx * cy
    groups = cy // 8
    place = [lax.axis_index(axis) for axis in AXES]
    rank = (place[0] * sizes[1] + place[1]) * sizes[2] + place[2]
    total = sizes[0] * sizes[1] * sizes[2]
    offsets = [o for o in itertools.product(*[range(n) for n in sizes]) if any(o)]

    def device_at(offset):
        return tuple(lax.rem(p + o % n, n) for p, o, n in zip(place, offset, sizes))

    barrier = pltpu.get_barrier_semaphore()
    for offset in offsets:
        pl.semaphore_signal(barrier, inc=1, device_id=device_at(offset), device_id_type=MESH)

    def lanes(rows):
        return lax.broadcasted_iota(jnp.int32, (rows, LANES), 1)

    def roll(v, n):
        n = n % LANES if isinstance(n, int) else n
        return v if isinstance(n, int) and n == 0 else pltpu.roll(v, n, 1)

    def back(x):
        return lax.rem(2 * LANES - 2 * x - 1, LANES)

    low = lanes(1) < HALF
    odd = lanes(1) % 2 == 1
    first = lanes(1) % HALF == 0
    end = lanes(1) % HALF == HALF - 1
    slot = lanes(cy) % HALF // 2

    def at(k, slab, row=0):
        return k * block + slab * pitch + row

    def inner(k, x):
        return pl.ds(pl.multiple_of(at(k, x + GHOST, PAD), 8), cy)

    def dense(k, x):
        return pl.ds(pl.multiple_of((k * cx + x) * cy, 8), cy)

    def plain(x):
        return pl.ds(pl.multiple_of(x * cy, 8), cy)

    def fold(v):
        return jnp.sum(v.reshape(groups, 8, LANES), axis=0)

    def sweep(body, pack=0, sums=0, unroll=UNROLL):
        zero = jnp.zeros((cy, LANES), jnp.float32)

        def step(x, carry):
            faces, gathered = carry
            (even_z, odd_z), terms = body(x)
            mixed = (jnp.where(first, even_z, odd_z), jnp.where(first, odd_z, even_z))[:pack] if pack else ()
            faces = tuple(jnp.where(slot == x, roll(m, 2 * x + 1), f) for m, f in zip(mixed, faces))
            return faces, tuple(a + fold(t) for a, t in zip(gathered, terms))

        start = (zero,) * pack, (jnp.zeros((8, LANES), jnp.float32),) * sums
        return lax.fori_loop(0, cx, step, start, unroll=unroll)

    def copies(e):
        deep = e in DEEP
        out = []

        def add(offset, src, dst):
            n = len(out)
            out.append(pltpu.make_async_remote_copy(
                src_ref=src, dst_ref=dst, send_sem=send_sem.at[e, n], recv_sem=recv_sem.at[e, n],
                device_id=device_at(offset), device_id_type=MESH))

        add((0, 0, -1), zsend.at[e, 0], zrecv.at[e, 0, PAD:PAD + cy])
        add((0, 0, 1), zsend.at[e, 1], zrecv.at[e, 1, PAD:PAD + cy])
        for k in range(2):
            for j in range(GHOST) if deep else (0,):
                add((-1, 0, 0), ext.at[e, pl.ds(at(k, GHOST + j, PAD), cy)],
                    ext.at[e, pl.ds(at(k, GHOST + cx + j, PAD), cy)])
                add((1, 0, 0), ext.at[e, pl.ds(at(k, GHOST + cx - 1 - j, PAD), cy)],
                    ext.at[e, pl.ds(at(k, GHOST - 1 - j, PAD), cy)])
        planes = slice(0, GHOST if deep else 1)
        for side in range(2):
            add((0, 2 * side - 1, 0), ysend.at[e, side, planes], yrecv.at[e, side, planes])
        if deep:
            for n, (a, b) in enumerate(itertools.product((-1, 1), repeat=2)):
                add((a, b, 0), xysend.at[e, n], xyrecv.at[e, n])
                add((a, 0, b), xzsend.at[e, n], xzrecv.at[e, n])
                tile = slice(0, 8) if a < 0 else slice(cy - 8, cy)
                into = slice(PAD + cy, 2 * PAD + cy) if a < 0 else slice(0, PAD)
                add((0, a, b), zsend.at[e, (b + 1) // 2, tile], zrecv.at[e, (b + 1) // 2, into])
        return out

    def send(e, faces):
        zown[e] = faces[0]
        if e in DEEP:
            zsend[e, 0] = jnp.where(odd, faces[0], roll(faces[1], -1))
            zsend[e, 1] = jnp.where(odd, roll(faces[1], 1), faces[0])
        else:
            zsend[e, 0] = faces[0]
            zsend[e, 1] = faces[0]
        for side in range(2):
            for plane in range(GHOST if e in DEEP else 1):
                y = cy - 1 - plane if side else plane
                for k in range(2):
                    ysend[e, side, plane, k * cx:(k + 1) * cx] = ext[e, pl.ds(at(k, GHOST, PAD + y), cx, stride=pitch), :]
        if e in DEEP:
            for n, (a, b) in enumerate(itertools.product((-1, 1), repeat=2)):
                for k in range(2):
                    row = at(k, GHOST + (cx - 1 if a > 0 else 0), PAD + (cy - 1 if b > 0 else 0))
                    xysend[e, n, k:k + 1] = ext[e, row:row + 1, :]
                lane = (2 * (cx - 1) if a > 0 else 0) + (0 if b > 0 else 1)
                packed = jnp.zeros((8, LANES), jnp.float32)
                for g in range(groups):
                    part = roll(zsend[e, (b + 1) // 2, 8 * g:8 * g + 8], 2 * g)
                    packed = jnp.where(lanes(8) % HALF == (lane + 2 * g) % HALF, part, packed)
                xzsend[e, n] = packed
        for copy in copies(e):
            copy.start()

    def arrive(e):
        for copy in copies(e):
            copy.wait()
        for side in range(2):
            for plane in range(GHOST if e in DEEP else 1):
                for k in range(2):
                    row = at(k, GHOST, PAD - 1 - plane if side else pitch + plane)
                    ext[e, pl.ds(row, cx, stride=pitch), :] = yrecv[e, side, plane, k * cx:(k + 1) * cx]
        if e not in DEEP:
            left, right = zrecv[e, 1, PAD:PAD + cy], zrecv[e, 0, PAD:PAD + cy]
            cp[PAD:] = jnp.where(odd, roll(left, HALF + 1), roll(right, HALF - 1))
            return
        left, right = zrecv[e, 1], zrecv[e, 0]
        ck[...] = jnp.where(odd, roll(left, HALF + 1), roll(right, HALF - 1))
        side_x = [[None, None], [None, None]]
        for n, (a, b) in enumerate(itertools.product((-1, 1), repeat=2)):
            for k in range(2):
                row = at(k, GHOST - 1 if a > 0 else GHOST + cx, PAD - 1 if b > 0 else pitch)
                ext[e, row:row + 1, :] = xyrecv[e, n, k:k + 1]
            lane = (2 * (cx - 1) if a > 0 else 0) + (0 if b > 0 else 1)
            shift = -(lane + HALF) if b > 0 else HALF - 1 - lane
            side_x[0 if a > 0 else 1][0 if b > 0 else 1] = [
                roll(xzrecv[e, n], shift - 2 * g) for g in range(groups)]
        for side in range(2):
            for g in range(groups):
                xe[side, 8 * g:8 * g + 8] = jnp.where(first, side_x[side][0][g], side_x[side][1][g])
        top = lax.broadcasted_iota(jnp.int32, (PAD, LANES), 0) == 0
        cp[0:PAD] = jnp.where(top, roll(ck[PAD + cy:], 2), ck[0:PAD])
        mid = ck[PAD:PAD + cy]
        cp[PAD:] = mid
        around = jnp.where(odd, roll(left[PAD:PAD + cy], HALF), roll(right[PAD:PAD + cy], HALF)) + zown[e]
        pos = lanes(1) % HALF
        around = around + jnp.where(pos < 2, roll(xe[0], 1), roll(mid, 2))
        around = around + jnp.where((pos >= 2 * cx - 2) & (pos < 2 * cx), roll(xe[1], 2 * cx - 1), roll(mid, -2))
        around = around + (ck[PAD - 1:PAD + cy - 1] + ck[PAD + 1:PAD + cy + 1])
        uz[...] = kz[...] * mid - around

    def apply(src, base, rows, edge):
        bases = [pl.multiple_of(base + k * block, 8) for k in range(2)]
        center = [src[pl.ds(b, rows), :] for b in bases]
        beside = [
            center[1] + jnp.where(first, edge, roll(center[1], 1)),
            center[0] + jnp.where(end, edge, roll(center[0], -1)),
        ]
        out = []
        for k, b in enumerate(bases):
            around = src[pl.ds(b + pitch, rows), :] + src[pl.ds(b - pitch, rows), :]
            around = around + (src[pl.ds(b + 1, rows), :] + src[pl.ds(b - 1, rows), :])
            out.append(ext[KAP, pl.ds(b, rows), :] * center[k] - (around + beside[k]))
        return out

    def wide(e):
        src, dst = ext.at[e], uext.at[e]

        def put(base, rows, edge):
            for k, v in enumerate(apply(src, base, rows, edge)):
                dst[pl.ds(pl.multiple_of(base + k * block, 8), rows), :] = v

        put(at(0, GHOST - 1, PAD), cy, xe[0])

        def step(x, carry):
            put(at(0, x + GHOST), pitch, roll(cp[...], back(x)))
            return carry
        lax.fori_loop(0, cx, step, 0, unroll=UNROLL)
        put(at(0, GHOST + cx, PAD), cy, xe[1])
        put(at(0, GHOST + cx), PAD, roll(cp[0:PAD], -2 * cx - 1))

    def again(e, x):
        return apply(uext.at[e], at(0, x + GHOST, PAD), cy, roll(uz[...], back(x)))

    def once(e, x):
        return apply(ext.at[e], at(0, x + GHOST, PAD), cy, roll(cp[PAD:], back(x)))

    def reduce_start(n, gathered):
        line = jnp.zeros((1, LANES), jnp.float32)
        for j, acc in enumerate(gathered):
            part = jnp.sum(acc, axis=0, keepdims=True)
            for s in range(sets):
                value = jnp.sum(jnp.where(low == (s == 0), part, 0.0), axis=1, keepdims=True)
                line = jnp.where(lanes(1) == 2 * s + j, value, line)
        red_out[n] = line
        red[n, rank] = line
        for offset in offsets:
            pltpu.make_async_remote_copy(
                src_ref=red_out.at[n], dst_ref=red.at[n, rank], send_sem=red_send.at[n],
                recv_sem=red_recv.at[n], device_id=device_at(offset), device_id_type=MESH).start()

    def spread(v, j):
        value = jnp.sum(jnp.where(lanes(1) == j, v, 0.0), axis=1, keepdims=True)
        return jnp.broadcast_to(value, (1, LANES))

    def reduce_end(n):
        many = red.at[n, pl.ds(0, total - 1)]
        pltpu.make_async_copy(many, many, red_recv.at[n]).wait()
        pltpu.make_async_copy(many, many, red_send.at[n]).wait()
        line = jnp.sum(red[n], axis=0)
        return [jnp.where(low, spread(line, j), spread(line, 2 + j)) for j in range(2)]

    def take(v, index):
        return jnp.take_along_axis(v, index, axis=1)

    lane = lanes(cy)
    split_low = 2 * (lane % HALF) + lane // HALF
    split_high = 2 * (lane % HALF) + 1 - lane // HALF
    join_low = lane // 2 + HALF * (lane % 2)
    join_high = lane // 2 + HALF * (1 - lane % 2)

    def split(ref, x):
        a, b = take(ref[0, plain(x), :], split_low), take(ref[1, plain(x), :], split_high)
        return jnp.where(low, a, b), roll(jnp.where(low, b, a), HALF)

    def join(even_z, odd_z):
        turned = roll(odd_z, HALF)
        return take(jnp.where(low, even_z, turned), join_low), take(jnp.where(low, turned, even_z), join_high)

    def keep(e, x, pair):
        for k in range(2):
            ext[e, inner(k, x), :] = pair[k]

    def load(e, ref):
        def body(x):
            pair = split(ref, x)
            keep(e, x, pair)
            return pair, ()
        return sweep(body, 2 if e in DEEP else 1)[0]

    def load_kap(x):
        value = 4.0 * jnp.exp(-2.0 * lr_ref[plain(x), :])
        kap[plain(x), :] = value
        a = take(value + 6.0, split_low)
        b = roll(a, HALF)
        pair = jnp.where(low, a, b), jnp.where(low, b, a)
        keep(KAP, x, pair)
        return pair, ()

    faces_start = load(X0, start_ref)
    faces_kap = sweep(load_kap, 1)[0]
    pl.semaphore_wait(barrier, total - 1)
    send(X0, faces_start)
    send(KAP, faces_kap)
    send(STATE, load(STATE, state_ref))

    upper = lines // 2
    for s in range(sets):
        cell = idx_ref[s]
        value = val_ref[s]
        top = value.astype(jnp.bfloat16).astype(jnp.float32)
        line = cell // cz
        key = line // upper * LANES + cell % cz
        col = lax.broadcasted_iota(jnp.int32, (2 * LANES, nobs), 0)
        half = col % LANES // HALF
        hit = key == col // LANES * LANES + 2 * (col % HALF) + (half if s == 0 else 1 - half)
        cols[0] = jnp.where(hit, 1.0, 0.0).astype(jnp.bfloat16)
        cols[1] = jnp.where(hit, top, 0.0).astype(jnp.bfloat16)
        cols[2] = jnp.where(hit, value - top, 0.0).astype(jnp.bfloat16)
        short = line % upper

        def rows_of(m, carry, short=short):
            ids = lax.broadcasted_iota(jnp.int32, (LANES, nobs), 0) + m * LANES
            hot[pl.ds(pl.multiple_of(m * LANES, LANES), LANES), :] = jnp.where(ids == short, 1.0, 0.0).astype(jnp.bfloat16)
            return carry
        lax.fori_loop(0, upper // LANES, rows_of, 0)

        def product(n):
            return lax.dot_general(hot[...], cols[n], (((1,), (1,)), ((), ())), preferred_element_type=jnp.float32)

        count = product(0) * (1.0 / noise_var)
        amount = (product(1) + product(2)) * (1.0 / noise_var)
        for h in range(2):
            raw[s, 0, h * upper:(h + 1) * upper] = count[:, h * LANES:(h + 1) * LANES]
            raw[s, 1, h * upper:(h + 1) * upper] = amount[:, h * LANES:(h + 1) * LANES]

    def mix(n, x):
        a, b = raw[0, n, plain(x), :], raw[1, n, plain(x), :]
        return jnp.where(low, a, b), roll(jnp.where(low, b, a), HALF)

    def right_pass(x):
        count, amount = mix(0, x), mix(1, x)
        for k in range(2):
            weight[dense(k, x), :] = count[k]
            rhs[dense(k, x), :] = amount[k] - count[k] * (ext[STATE, inner(k, x), :] + ext[X0, inner(k, x), :])
        return (None, None), ()

    sweep(right_pass)
    arrive(KAP)
    kz[...] = cp[PAD:]
    arrive(X0)
    wide(X0)

    def residual_pass(x):
        out = again(X0, x)
        pair = [rhs[dense(k, x), :] - out[k] for k in range(2)]
        keep(R0, x, pair)
        return pair, ()

    send(R0, sweep(residual_pass, 2)[0])

    arrive(STATE)

    def state_pass(x):
        out = once(STATE, x)
        for k in range(2):
            ast[dense(k, x), :] = out[k]
        return (None, None), ()

    sweep(state_pass)

    arrive(R0)
    wide(R0)

    def image_pass(x):
        out = again(R0, x)
        now = [ext[R0, inner(k, x), :] for k in range(2)]
        pair = [out[k] + weight[dense(k, x), :] * now[k] for k in range(2)]
        keep(W0, x, pair)
        return pair, (now[0] * now[0] + now[1] * now[1], now[0] * pair[0] + now[1] * pair[1])

    faces, gathered = sweep(image_pass, 2, 2)
    send(W0, faces)
    reduce_start(0, gathered)

    norms, steps, ratios = [], [], []
    for k, e in enumerate((W0, W1)):
        arrive(e)
        wide(e)

        def next_image(x, e=e):
            out = again(e, x)
            for p in range(2):
                q[dense(p, x), :] = out[p] + weight[dense(p, x), :] * ext[e, inner(p, x), :]
            return (None, None), ()

        sweep(next_image)
        norm, product = reduce_end(k)
        if k == 0:
            ratio, step_size = None, norm / product
        else:
            ratio = norm / norms[-1]
            step_size = norm / (product - ratio * norm / steps[-1])
        norms.append(norm)
        steps.append(step_size)
        ratios.append(ratio)

        def update(x, k=k, e=e, ratio=ratio, step_size=step_size):
            pair, terms = [], []
            for p in range(2):
                here, there = dense(p, x), inner(p, x)
                image, vec = q[here, :], ext[e, there, :]
                if k == 0:
                    z[here, :] = image
                    follow, now = vec, ext[R0, there, :]
                else:
                    image = image + ratio * z[here, :]
                    follow, now = vec + ratio * ext[W0, there, :], r[k - 1, here, :]
                    s_buf[here, :] = follow
                vec = vec - step_size * image
                now = now - step_size * follow
                ext[e + 1, there, :] = vec
                r[k, here, :] = now
                pair.append(vec)
                terms.append((now * now, now * vec))
            return pair, (terms[0][0] + terms[1][0], terms[0][1] + terms[1][1])

        faces, gathered = sweep(update, 2 if e + 1 in DEEP else 1, 2)
        send(e + 1, faces)
        reduce_start(k + 1, gathered)

        def trail(x, k=k, ratio=ratio, step_size=step_size):
            for p in range(2):
                here, there = dense(p, x), inner(p, x)
                if k == 0:
                    xs[here, :] = ext[X0, there, :] + step_size * ext[R0, there, :]
                    now = uext[R0, there, :]
                    axs[here, :] = uext[X0, there, :] + step_size * now
                    ar[0, here, :] = now - step_size * uext[W0, there, :]
                else:
                    toward = r[0, here, :] + ratio * ext[R0, there, :]
                    d[here, :] = toward
                    xs[here, :] = xs[here, :] + step_size * toward
                    now = ar[0, here, :]
                    toward = now + ratio * uext[R0, there, :]
                    ad[here, :] = toward
                    axs[here, :] = axs[here, :] + step_size * toward
                    follow = uext[W1, there, :] + ratio * uext[W0, there, :]
                    q[here, :] = follow
                    ar[1, here, :] = now - step_size * follow
            return (None, None), ()

        sweep(trail)

    arrive(W2)

    def last_half(x):
        out = once(W2, x)
        for p in range(2):
            z[dense(p, x), :] = out[p]
        return (None, None), ()

    sweep(last_half)
    norm, product = reduce_end(2)
    ratio = norm / norms[-1]
    step_size = norm / (product - ratio * norm / steps[-1])

    def last_residual(x):
        norm_terms, terms = [], []
        for p in range(2):
            here, there = dense(p, x), inner(p, x)
            now = r[1, here, :] - step_size * (ext[W2, there, :] + ratio * s_buf[here, :])
            inner_now = ar[1, here, :] - step_size * (z[here, :] + ratio * q[here, :])
            r[2, here, :] = now
            ar[2, here, :] = inner_now
            norm_terms.append(now * now)
            terms.append(inner_now * inner_now + weight[here, :] * now * now)
        return (None, None), (norm_terms[0] + norm_terms[1], terms[0] + terms[1])

    reduce_start(3, sweep(last_residual, 0, 2)[1])

    def prepare(x):
        towards, olds, nows, grads = [], [], [], []
        for p in range(2):
            here, there = dense(p, x), inner(p, x)
            field, image = ext[STATE, there, :], ast[here, :]
            toward = r[1, here, :] + ratio * d[here, :]
            applied = ar[1, here, :] + ratio * ad[here, :]
            old = xs[here, :] + step_size * toward
            old_applied = axs[here, :] + step_size * applied
            now, now_applied = r[2, here, :], ar[2, here, :]
            towards.append(toward)
            olds.append(old)
            nows.append(now)
            grads.append((
                old * image + old_applied * field,
                now * image + now_applied * field,
                toward * image + applied * field,
            ))
        here = plain(x)
        scale = -2.0 * kap[here, :]
        for ref, pair in ((xn, olds), (rn, nows), (dn, towards)):
            for s, v in enumerate(join(*pair)):
                ref[s, here, :] = v
        parts = [join(grads[0][n], grads[1][n]) for n in range(3)]
        gx[here, :] = scale * (parts[0][0] + parts[0][1])
        for s in range(sets):
            gr[s, here, :] = scale * parts[1][s]
            gd[s, here, :] = scale * parts[2][s]
        return (None, None), ()

    sweep(prepare, unroll=4)
    last_norm, last_product = reduce_end(3)
    last_ratio = last_norm / norm
    last_step = last_norm / (last_product - last_ratio * last_norm / step_size)
    last_both = last_step * last_ratio
    one = [spread(last_step, s * HALF) for s in range(sets)]
    two = [spread(last_both, s * HALF) for s in range(sets)]

    def finish(x, carry):
        here = plain(x)
        grad = gx[here, :]
        for s in range(sets):
            adj_ref[s, here, :] = xn[s, here, :] + (one[s] * rn[s, here, :] + two[s] * dn[s, here, :])
            grad = grad + (one[s] * gr[s, here, :] + two[s] * gd[s, here, :])
        grad_ref[here, :] = grad
        return carry
    lax.fori_loop(0, cx, finish, 0, unroll=UNROLL)


def on_device(sizes, log_range, state, adjoint_start, obs_index, obs_value):
    sets, cx, cy, cz = state.shape
    nobs = obs_index.shape[-1]
    rows = cx * cy
    total = sizes[0] * sizes[1] * sizes[2]
    whole = 2 * (cx + 2 * GHOST) * (cy + PAD) + 8
    f32 = jnp.float32
    field = pltpu.VMEM((2 * rows, LANES), f32)
    natural = pltpu.VMEM((sets, rows, cz), f32)
    vmem = pl.BlockSpec(memory_space=pltpu.VMEM)
    gradient, adjoint = pl.pallas_call(
        functools.partial(kernel, sizes, (sets, cx, cy, cz, nobs)),
        out_shape=(
            jax.ShapeDtypeStruct((rows, cz), jnp.float32),
            jax.ShapeDtypeStruct((sets, rows, cz), jnp.float32),
        ),
        in_specs=[vmem] * 5,
        out_specs=(vmem, vmem),
        scratch_shapes=[
            pltpu.VMEM((FIELDS, whole, LANES), f32),
            pltpu.VMEM((len(DEEP), whole, LANES), f32),
            pltpu.VMEM((FIELDS, 2, GHOST, 2 * cx, LANES), f32),
            pltpu.VMEM((FIELDS, 2, GHOST, 2 * cx, LANES), f32),
            pltpu.VMEM((FIELDS, 2, cy, LANES), f32),
            pltpu.VMEM((FIELDS, 2, cy + 2 * PAD, LANES), f32),
            pltpu.VMEM((FIELDS, cy, LANES), f32),
            *[pltpu.VMEM((len(DEEP), 4, 8, LANES), f32)] * 4,
            pltpu.VMEM((cy + 2 * PAD, LANES), f32),
            pltpu.VMEM((cy + PAD, LANES), f32),
            pltpu.VMEM((2, cy, LANES), f32),
            pltpu.VMEM((cy, LANES), f32),
            pltpu.VMEM((cy, LANES), f32),
            pltpu.VMEM((rows, cz), f32),
            pltpu.VMEM((rows // 2, nobs), jnp.bfloat16),
            pltpu.VMEM((3, 2 * LANES, nobs), jnp.bfloat16),
            pltpu.VMEM((sets, 2, rows, LANES), f32),
            field, field, field, field,
            pltpu.VMEM((3, 2 * rows, LANES), f32),
            pltpu.VMEM((3, 2 * rows, LANES), f32),
            *[field] * 6,
            natural, natural, natural,
            pltpu.VMEM((rows, cz), f32),
            natural, natural,
            pltpu.VMEM((ITERS, 1, LANES), f32),
            pltpu.VMEM((ITERS, total, 1, LANES), f32),
            pltpu.SemaphoreType.DMA((FIELDS, COPIES)),
            pltpu.SemaphoreType.DMA((FIELDS, COPIES)),
            pltpu.SemaphoreType.DMA((ITERS,)),
            pltpu.SemaphoreType.DMA((ITERS,)),
        ],
        compiler_params=pltpu.CompilerParams(
            collective_id=0, has_side_effects=True, vmem_limit_bytes=63 * 1024 * 1024
        ),
    )(
        log_range.reshape(rows, cz),
        state.reshape(sets, rows, cz),
        adjoint_start.reshape(sets, rows, cz),
        obs_index.reshape(sets, 1, nobs),
        obs_value.reshape(sets, 1, nobs),
    )
    return gradient.reshape(cx, cy, cz), adjoint.reshape(sets, cx, cy, cz)


def solution(mesh):
    in_specs = (
        P("gx", "gy", "gz"),
        P(None, "gx", "gy", "gz"),
        P(None, "gx", "gy", "gz"),
        P(None, "gx", "gy", "gz", None),
        P(None, "gx", "gy", "gz", None),
    )
    out_specs = (P("gx", "gy", "gz"), P(None, "gx", "gy", "gz"))
    sizes = tuple(mesh.shape[axis] for axis in AXES)
    return jax.shard_map(
        functools.partial(on_device, sizes), mesh=mesh, in_specs=in_specs, out_specs=out_specs, check_vma=False
    )
```

time: 96 us -> 82.2 us (0.86)
  Pallas kernels: 90.1 us -> 78.5 us
  local copies, waits for them, and re-layouts: 4.98 us -> 2.93 us
    pallas_call x1, Pallas kernels: 90.1 us -> 78.5 us  [on_device(): pl.pallas_call(functools.partial(kernel, sizes, (sets, cx, cy, cz, nobs))...]
    unnamed x8 -> x4, local copies, waits for them, and re-layouts: 4.98 us -> 2.93 us
where the time goes in v1:
time: 82.2 us; the launch traced here: 82.1 us
  Pallas kernels  78.5 us (95%)
  local copies, waits for them, and re-layouts  2.93 us (4%)
    pallas_call x1, Pallas kernels, on_device(): pl.pallas_call(functools.partial(kernel, sizes, (sets, cx, cy, cz, nobs))...  78.5 us
    unnamed x4, local copies, waits for them, and re-layouts  2.93 us

profile of v1, /device:TPU:0, one launch (start us, length us, event | category | flops | bytes accessed | tf_op | source)
XLA Modules:
  0.0 82.1 jit_solution(15104195718146254946)
XLA Ops:
  0.6 78.5 %shard_map.68 = (f32[1024,128]{1,0:T(8,128)}, f32[2,1024,128]{2,1,0:T(8,128)}) custom-call(f32[1024,128]{1,0:T(8,128)} %bitcast.11, f32[2,1024,128]{2,1,0:T(8,128)} %bitcast.8, f32[2,1024,128]{2,1,0:T(8,128)} %bitcast.9, s32[2,1,4096]{2,1,0:T(1,128)} %bitcast.12, f32[2,1,4096]{2,1,0:T(1,128)} %bitcast.13), custom_call_target="tpu_custom_call" | custom-call | tf_op jit(solution)/shard_map/pallas_call | solution.py:527
  79.1 0.0 copy-start
  79.1 2.0 %copy.9 = f32[32,32,128]{2,1,0:T(8,128)} copy(f32[32,32,128]{2,1,0:T(8,128)} %bitcast.10) | data formatting | bytes 1048576
  81.1 0.0 copy-done
  81.1 1.0 %copy.10 = f32[2,32,32,128]{3,2,1,0:T(8,128)} copy(f32[2,32,32,128]{3,2,1,0:T(8,128)S(1)} %bitcast.7) | data formatting | bytes 2097152
Async XLA Ops:
  79.1 2.0 %copy-start = (f32[2,1024,128]{2,1,0:T(8,128)S(1)}, f32[2,1024,128]{2,1,0:T(8,128)}, u32[]{:S(2)}) copy-start(f32[2,1024,128]{2,1,0:T(8,128)} %get-tuple-element.5) | copy-start | bytes 3145732

commit v2 on v1

--- a/solution.py
+++ b/solution.py
@@ -24,10 +24,10 @@
 
 
 def kernel(
-    sizes, dims, lr_ref, state_ref, start_ref, idx_ref, val_ref, grad_ref, adj_ref,
-    ext, uext, ysend, yrecv, zsend, zrecv, zown, xysend, xyrecv, xzsend, xzrecv,
-    ck, cp, xe, uz, kz, kap, hot, cols, raw, weight, rhs, z, s_buf, r, ar, q, ast, d, ad, xs, axs,
-    xn, rn, dn, gx, gr, gd, red_out, red, send_sem, recv_sem, red_send, red_recv,
+    sizes, dims, lr_hbm, state_hbm, start_hbm, idx_hbm, val_hbm, grad_ref, adj_ref,
+    lr_ref, state_ref, start_ref, idx_ref, val_ref, ext, uext, ysend, yrecv, zsend, zrecv, zown, xysend, xyrecv, xzsend, xzrecv,
+    ck, cp, xe, uz, kz, kap, cols, raw, weight, rhs, z, s_buf, r, ar, q, ast, ad, xs, axs,
+    gr, gd, red_out, red, send_sem, recv_sem, red_send, red_recv, load_sem,
 ):
     sets, cx, cy, cz, nobs = dims
     pitch = cy + PAD
@@ -47,6 +47,11 @@
     for offset in offsets:
         pl.semaphore_signal(barrier, inc=1, device_id=device_at(offset), device_id_type=MESH)
 
+    pairs = ((start_hbm, start_ref), (idx_hbm, idx_ref), (val_hbm, val_ref), (lr_hbm, lr_ref), (state_hbm, state_ref))
+    loads = [pltpu.make_async_copy(a, b, load_sem.at[n]) for n, (a, b) in enumerate(pairs)]
+    for copy in loads:
+        copy.start()
+
     def lanes(rows):
         return lax.broadcasted_iota(jnp.int32, (rows, LANES), 1)
 
@@ -78,7 +83,7 @@
     def fold(v):
         return jnp.sum(v.reshape(groups, 8, LANES), axis=0)
 
-    def sweep(body, pack=0, sums=0, unroll=UNROLL):
+    def sweep(body, pack=0, sums=0, unroll=UNROLL, early=None):
         zero = jnp.zeros((cy, LANES), jnp.float32)
 
         def step(x, carry):
@@ -89,7 +94,12 @@
             return faces, tuple(a + fold(t) for a, t in zip(gathered, terms))
 
         start = (zero,) * pack, (jnp.zeros((8, LANES), jnp.float32),) * sums
-        return lax.fori_loop(0, cx, step, start, unroll=unroll)
+        if early is None:
+            return lax.fori_loop(0, cx, step, start, unroll=unroll)
+        for x in (*range(GHOST), *range(cx - GHOST, cx)):
+            start = step(x, start)
+        send_x(early)
+        return lax.fori_loop(GHOST, cx - GHOST, step, start, unroll=7)
 
     def copies(e):
         deep = e in DEEP
@@ -101,14 +111,15 @@
                 src_ref=src, dst_ref=dst, send_sem=send_sem.at[e, n], recv_sem=recv_sem.at[e, n],
                 device_id=device_at(offset), device_id_type=MESH))
 
-        add((0, 0, -1), zsend.at[e, 0], zrecv.at[e, 0, PAD:PAD + cy])
-        add((0, 0, 1), zsend.at[e, 1], zrecv.at[e, 1, PAD:PAD + cy])
         for k in range(2):
             for j in range(GHOST) if deep else (0,):
                 add((-1, 0, 0), ext.at[e, pl.ds(at(k, GHOST + j, PAD), cy)],
                     ext.at[e, pl.ds(at(k, GHOST + cx + j, PAD), cy)])
                 add((1, 0, 0), ext.at[e, pl.ds(at(k, GHOST + cx - 1 - j, PAD), cy)],
                     ext.at[e, pl.ds(at(k, GHOST - 1 - j, PAD), cy)])
+        near = len(out)
+        add((0, 0, -1), zsend.at[e, 0], zrecv.at[e, 0, PAD:PAD + cy])
+        add((0, 0, 1), zsend.at[e, 1], zrecv.at[e, 1, PAD:PAD + cy])
         planes = slice(0, GHOST if deep else 1)
         for side in range(2):
             add((0, 2 * side - 1, 0), ysend.at[e, side, planes], yrecv.at[e, side, planes])
@@ -119,7 +130,11 @@
                 tile = slice(0, 8) if a < 0 else slice(cy - 8, cy)
                 into = slice(PAD + cy, 2 * PAD + cy) if a < 0 else slice(0, PAD)
                 add((0, a, b), zsend.at[e, (b + 1) // 2, tile], zrecv.at[e, (b + 1) // 2, into])
-        return out
+        return out[:near], out[near:]
+
+    def send_x(e):
+        for copy in copies(e)[0]:
+            copy.start()
 
     def send(e, faces):
         zown[e] = faces[0]
@@ -145,11 +160,11 @@
                     part = roll(zsend[e, (b + 1) // 2, 8 * g:8 * g + 8], 2 * g)
                     packed = jnp.where(lanes(8) % HALF == (lane + 2 * g) % HALF, part, packed)
                 xzsend[e, n] = packed
-        for copy in copies(e):
+        for copy in copies(e)[1]:
             copy.start()
 
     def arrive(e):
-        for copy in copies(e):
+        for copy in sum(copies(e), []):
             copy.wait()
         for side in range(2):
             for plane in range(GHOST if e in DEEP else 1):
@@ -250,24 +265,31 @@
         return jnp.take_along_axis(v, index, axis=1)
 
     lane = lanes(cy)
-    split_low = 2 * (lane % HALF) + lane // HALF
-    split_high = 2 * (lane % HALF) + 1 - lane // HALF
-    join_low = lane // 2 + HALF * (lane % 2)
-    join_high = lane // 2 + HALF * (1 - lane % 2)
+    apart = 2 * (lane % HALF) + lane // HALF
+    together = lane // 2 + HALF * (lane % 2)
+
+    def permute(ref, index, rows):
+        def step(m, carry):
+            here = pl.ds(pl.multiple_of(m * cy, 8), cy)
+            ref[here, :] = take(ref[here, :], index)
+            return carry
+        lax.fori_loop(0, rows // cy, step, 0, unroll=2 * UNROLL)
 
     def split(ref, x):
-        a, b = take(ref[0, plain(x), :], split_low), take(ref[1, plain(x), :], split_high)
-        return jnp.where(low, a, b), roll(jnp.where(low, b, a), HALF)
+        a, b = ref[0, plain(x), :], ref[1, plain(x), :]
+        return jnp.where(low, a, roll(b, HALF)), jnp.where(low, roll(a, HALF), b)
 
     def join(even_z, odd_z):
-        turned = roll(odd_z, HALF)
-        return take(jnp.where(low, even_z, turned), join_low), take(jnp.where(low, turned, even_z), join_high)
+        return jnp.where(low, even_z, roll(odd_z, HALF)), jnp.where(low, roll(even_z, HALF), odd_z)
 
     def keep(e, x, pair):
         for k in range(2):
             ext[e, inner(k, x), :] = pair[k]
 
     def load(e, ref):
+        for s in range(sets):
+            permute(ref.at[s], apart, lines)
+
         def body(x):
             pair = split(ref, x)
             keep(e, x, pair)
@@ -277,21 +299,15 @@
     def load_kap(x):
         value = 4.0 * jnp.exp(-2.0 * lr_ref[plain(x), :])
         kap[plain(x), :] = value
-        a = take(value + 6.0, split_low)
+        a = value + 6.0
         b = roll(a, HALF)
         pair = jnp.where(low, a, b), jnp.where(low, b, a)
         keep(KAP, x, pair)
         return pair, ()
 
-    faces_start = load(X0, start_ref)
-    faces_kap = sweep(load_kap, 1)[0]
-    pl.semaphore_wait(barrier, total - 1)
-    send(X0, faces_start)
-    send(KAP, faces_kap)
-    send(STATE, load(STATE, state_ref))
-
     upper = lines // 2
-    for s in range(sets):
+
+    def observe(s):
         cell = idx_ref[s]
         value = val_ref[s]
         top = value.astype(jnp.bfloat16).astype(jnp.float32)
@@ -300,25 +316,42 @@
         col = lax.broadcasted_iota(jnp.int32, (2 * LANES, nobs), 0)
         half = col % LANES // HALF
         hit = key == col // LANES * LANES + 2 * (col % HALF) + (half if s == 0 else 1 - half)
-        cols[0] = jnp.where(hit, 1.0, 0.0).astype(jnp.bfloat16)
-        cols[1] = jnp.where(hit, top, 0.0).astype(jnp.bfloat16)
-        cols[2] = jnp.where(hit, value - top, 0.0).astype(jnp.bfloat16)
+        for n, part in enumerate((1.0, top, value - top)):
+            cols[2 * LANES * n:2 * LANES * (n + 1)] = jnp.where(hit, part, 0.0).astype(jnp.bfloat16)
         short = line % upper
 
-        def rows_of(m, carry, short=short):
-            ids = lax.broadcasted_iota(jnp.int32, (LANES, nobs), 0) + m * LANES
-            hot[pl.ds(pl.multiple_of(m * LANES, LANES), LANES), :] = jnp.where(ids == short, 1.0, 0.0).astype(jnp.bfloat16)
+        def step(m, carry):
+            ids = lax.broadcasted_iota(jnp.int32, (upper, nobs), 0) + m * upper
+            hot = jnp.where(ids == short, 1.0, 0.0).astype(jnp.bfloat16)
+            got = lax.dot_general(hot, cols[...], (((1,), (1,)), ((), ())), preferred_element_type=jnp.float32)
+            count = got[:, :2 * LANES] * (1.0 / noise_var)
+            amount = (got[:, 2 * LANES:4 * LANES] + got[:, 4 * LANES:]) * (1.0 / noise_var)
+            for h in range(2):
+                here = pl.ds(pl.multiple_of(m * upper + h * upper, upper), upper)
+                raw[s, 0, here, :] = count[:, h * LANES:(h + 1) * LANES]
+                raw[s, 1, here, :] = amount[:, h * LANES:(h + 1) * LANES]
             return carry
-        lax.fori_loop(0, upper // LANES, rows_of, 0)
-
-        def product(n):
-            return lax.dot_general(hot[...], cols[n], (((1,), (1,)), ((), ())), preferred_element_type=jnp.float32)
-
-        count = product(0) * (1.0 / noise_var)
-        amount = (product(1) + product(2)) * (1.0 / noise_var)
-        for h in range(2):
-            raw[s, 0, h * upper:(h + 1) * upper] = count[:, h * LANES:(h + 1) * LANES]
-            raw[s, 1, h * upper:(h + 1) * upper] = amount[:, h * LANES:(h + 1) * LANES]
+
+        lax.fori_loop(0, 1, step, 0)
+
+    loads[0].wait()
+    faces_start = load(X0, start_ref)
+    loads[1].wait()
+    loads[2].wait()
+    observe(0)
+    loads[3].wait()
+    permute(lr_ref, apart, lines)
+    faces_kap = sweep(load_kap, 1)[0]
+    pl.semaphore_wait(barrier, total - 1)
+    send_x(X0)
+    send(X0, faces_start)
+    send_x(KAP)
+    send(KAP, faces_kap)
+    loads[4].wait()
+    faces_state = load(STATE, state_ref)
+    send_x(STATE)
+    send(STATE, faces_state)
+    observe(1)
 
     def mix(n, x):
         a, b = raw[0, n, plain(x), :], raw[1, n, plain(x), :]
@@ -343,7 +376,7 @@
         keep(R0, x, pair)
         return pair, ()
 
-    send(R0, sweep(residual_pass, 2)[0])
+    send(R0, sweep(residual_pass, 2, early=R0)[0])
 
     arrive(STATE)
 
@@ -365,7 +398,7 @@
         keep(W0, x, pair)
         return pair, (now[0] * now[0] + now[1] * now[1], now[0] * pair[0] + now[1] * pair[1])
 
-    faces, gathered = sweep(image_pass, 2, 2)
+    faces, gathered = sweep(image_pass, 2, 2, early=W0)
     send(W0, faces)
     reduce_start(0, gathered)
 
@@ -411,7 +444,7 @@
                 terms.append((now * now, now * vec))
             return pair, (terms[0][0] + terms[1][0], terms[0][1] + terms[1][1])
 
-        faces, gathered = sweep(update, 2 if e + 1 in DEEP else 1, 2)
+        faces, gathered = sweep(update, 2 if e + 1 in DEEP else 1, 2, early=e + 1)
         send(e + 1, faces)
         reduce_start(k + 1, gathered)
 
@@ -425,7 +458,7 @@
                     ar[0, here, :] = now - step_size * uext[W0, there, :]
                 else:
                     toward = r[0, here, :] + ratio * ext[R0, there, :]
-                    d[here, :] = toward
+                    rhs[here, :] = toward
                     xs[here, :] = xs[here, :] + step_size * toward
                     now = ar[0, here, :]
                     toward = now + ratio * uext[R0, there, :]
@@ -470,7 +503,7 @@
         for p in range(2):
             here, there = dense(p, x), inner(p, x)
             field, image = ext[STATE, there, :], ast[here, :]
-            toward = r[1, here, :] + ratio * d[here, :]
+            toward = r[1, here, :] + ratio * rhs[here, :]
             applied = ar[1, here, :] + ratio * ad[here, :]
             old = xs[here, :] + step_size * toward
             old_applied = axs[here, :] + step_size * applied
@@ -485,17 +518,26 @@
             ))
         here = plain(x)
         scale = -2.0 * kap[here, :]
-        for ref, pair in ((xn, olds), (rn, nows), (dn, towards)):
+        for s, v in enumerate(join(*olds)):
+            adj_ref[s, here, :] = v
+        for n, pair in enumerate((nows, towards)):
             for s, v in enumerate(join(*pair)):
-                ref[s, here, :] = v
+                raw[s, n, here, :] = v
         parts = [join(grads[0][n], grads[1][n]) for n in range(3)]
-        gx[here, :] = scale * (parts[0][0] + parts[0][1])
+        grad_ref[here, :] = scale * (parts[0][0] + parts[0][1])
         for s in range(sets):
             gr[s, here, :] = scale * parts[1][s]
             gd[s, here, :] = scale * parts[2][s]
         return (None, None), ()
 
     sweep(prepare, unroll=4)
+    for s in range(sets):
+        permute(adj_ref.at[s], together, lines)
+        for n in range(2):
+            permute(raw.at[s, n], together, lines)
+        permute(gr.at[s], together, lines)
+        permute(gd.at[s], together, lines)
+    permute(grad_ref, together, lines)
     last_norm, last_product = reduce_end(3)
     last_ratio = last_norm / norm
     last_step = last_norm / (last_product - last_ratio * last_norm / step_size)
@@ -505,9 +547,9 @@
 
     def finish(x, carry):
         here = plain(x)
-        grad = gx[here, :]
+        grad = grad_ref[here, :]
         for s in range(sets):
-            adj_ref[s, here, :] = xn[s, here, :] + (one[s] * rn[s, here, :] + two[s] * dn[s, here, :])
+            adj_ref[s, here, :] = adj_ref[s, here, :] + (one[s] * raw[s, 0, here, :] + two[s] * raw[s, 1, here, :])
             grad = grad + (one[s] * gr[s, here, :] + two[s] * gd[s, here, :])
         grad_ref[here, :] = grad
         return carry
@@ -530,9 +572,14 @@
             jax.ShapeDtypeStruct((rows, cz), jnp.float32),
             jax.ShapeDtypeStruct((sets, rows, cz), jnp.float32),
         ),
-        in_specs=[vmem] * 5,
+        in_specs=[pl.BlockSpec(memory_space=pltpu.HBM)] * 5,
         out_specs=(vmem, vmem),
         scratch_shapes=[
+            pltpu.VMEM((rows, cz), f32),
+            natural,
+            natural,
+            pltpu.VMEM((sets, 1, nobs), jnp.int32),
+            pltpu.VMEM((sets, 1, nobs), f32),
             pltpu.VMEM((FIELDS, whole, LANES), f32),
             pltpu.VMEM((len(DEEP), whole, LANES), f32),
             pltpu.VMEM((FIELDS, 2, GHOST, 2 * cx, LANES), f32),
@@ -547,15 +594,12 @@
             pltpu.VMEM((cy, LANES), f32),
             pltpu.VMEM((cy, LANES), f32),
             pltpu.VMEM((rows, cz), f32),
-            pltpu.VMEM((rows // 2, nobs), jnp.bfloat16),
-            pltpu.VMEM((3, 2 * LANES, nobs), jnp.bfloat16),
+            pltpu.VMEM((6 * LANES, nobs), jnp.bfloat16),
             pltpu.VMEM((sets, 2, rows, LANES), f32),
             field, field, field, field,
             pltpu.VMEM((3, 2 * rows, LANES), f32),
             pltpu.VMEM((3, 2 * rows, LANES), f32),
-            *[field] * 6,
-            natural, natural, natural,
-            pltpu.VMEM((rows, cz), f32),
+            *[field] * 5,
             natural, natural,
             pltpu.VMEM((ITERS, 1, LANES), f32),
             pltpu.VMEM((ITERS, total, 1, LANES), f32),
@@ -563,6 +607,7 @@
             pltpu.SemaphoreType.DMA((FIELDS, COPIES)),
             pltpu.SemaphoreType.DMA((ITERS,)),
             pltpu.SemaphoreType.DMA((ITERS,)),
+            pltpu.SemaphoreType.DMA((5,)),
         ],
         compiler_params=pltpu.CompilerParams(
             collective_id=0, has_side_effects=True, vmem_limit_bytes=63 * 1024 * 1024

time: 82.2 us -> 69.1 us (0.84)
  Pallas kernels: 78.5 us -> 65.3 us
    pallas_call x1, Pallas kernels: 78.5 us -> 65.3 us  [on_device(): pl.pallas_call(functools.partial(kernel, sizes, (sets, cx, cy, cz, nobs))...]
where the time goes in v2:
time: 69.1 us; the launch traced here: 68.9 us
  Pallas kernels  65.3 us (95%)
  local copies, waits for them, and re-layouts  2.93 us (4%)
    pallas_call x1, Pallas kernels, on_device(): pl.pallas_call(functools.partial(kernel, sizes, (sets, cx, cy, cz, nobs))...  65.3 us
    unnamed x4, local copies, waits for them, and re-layouts  2.93 us

profile of v2, /device:TPU:0, one launch (start us, length us, event | category | flops | bytes accessed | tf_op | source)
XLA Modules:
  0.0 68.9 jit_solution(2082850395624691967)
XLA Ops:
  0.6 65.3 %shard_map.68 = (f32[1024,128]{1,0:T(8,128)}, f32[2,1024,128]{2,1,0:T(8,128)}) custom-call(f32[1024,128]{1,0:T(8,128)} %bitcast.11, f32[2,1024,128]{2,1,0:T(8,128)} %bitcast.8, f32[2,1024,128]{2,1,0:T(8,128)} %bitcast.9, s32[2,1,4096]{2,1,0:T(1,128)} %bitcast.12, f32[2,1,4096]{2,1,0:T(1,128)} %bitcast.13), custom_call_target="tpu_custom_call" | custom-call | tf_op jit(solution)/shard_map/pallas_call | solution.py:569
  66.0 0.0 copy-start
  66.0 2.0 %copy.9 = f32[32,32,128]{2,1,0:T(8,128)} copy(f32[32,32,128]{2,1,0:T(8,128)} %bitcast.10) | data formatting | bytes 1048576
  68.0 0.0 copy-done
  68.0 1.0 %copy.10 = f32[2,32,32,128]{3,2,1,0:T(8,128)} copy(f32[2,32,32,128]{3,2,1,0:T(8,128)S(1)} %bitcast.7) | data formatting | bytes 2097152
Async XLA Ops:
  66.0 2.0 %copy-start = (f32[2,1024,128]{2,1,0:T(8,128)S(1)}, f32[2,1024,128]{2,1,0:T(8,128)}, u32[]{:S(2)}) copy-start(f32[2,1024,128]{2,1,0:T(8,128)} %get-tuple-element.5) | copy-start | bytes 3145732

commit v3 on v2

--- a/solution.py
+++ b/solution.py
@@ -336,9 +336,6 @@
 
     loads[0].wait()
     faces_start = load(X0, start_ref)
-    loads[1].wait()
-    loads[2].wait()
-    observe(0)
     loads[3].wait()
     permute(lr_ref, apart, lines)
     faces_kap = sweep(load_kap, 1)[0]
@@ -351,6 +348,9 @@
     faces_state = load(STATE, state_ref)
     send_x(STATE)
     send(STATE, faces_state)
+    loads[1].wait()
+    loads[2].wait()
+    observe(0)
     observe(1)
 
     def mix(n, x):

time: 69.1 us -> 62.4 us (0.903)
  Pallas kernels: 65.3 us -> 58.7 us
    pallas_call x1, Pallas kernels: 65.3 us -> 58.7 us  [on_device(): pl.pallas_call(functools.partial(kernel, sizes, (sets, cx, cy, cz, nobs))...]
where the time goes in v3:
time: 62.4 us; the launch traced here: 62.2 us
  Pallas kernels  58.7 us (94%)
  local copies, waits for them, and re-layouts  2.93 us (5%)
  between operations  0.65 us (1%)
    pallas_call x1, Pallas kernels, on_device(): pl.pallas_call(functools.partial(kernel, sizes, (sets, cx, cy, cz, nobs))...  58.7 us
    unnamed x4, local copies, waits for them, and re-layouts  2.93 us

profile of v3, /device:TPU:0, one launch (start us, length us, event | category | flops | bytes accessed | tf_op | source)
XLA Modules:
  0.0 62.2 jit_solution(2335823845188011471)
XLA Ops:
  0.6 58.7 %shard_map.68 = (f32[1024,128]{1,0:T(8,128)}, f32[2,1024,128]{2,1,0:T(8,128)}) custom-call(f32[1024,128]{1,0:T(8,128)} %bitcast.11, f32[2,1024,128]{2,1,0:T(8,128)} %bitcast.8, f32[2,1024,128]{2,1,0:T(8,128)} %bitcast.9, s32[2,1,4096]{2,1,0:T(1,128)} %bitcast.12, f32[2,1,4096]{2,1,0:T(1,128)} %bitcast.13), custom_call_target="tpu_custom_call" | custom-call | tf_op jit(solution)/shard_map/pallas_call | solution.py:569
  59.3 0.0 copy-start
  59.3 2.0 %copy.9 = f32[32,32,128]{2,1,0:T(8,128)} copy(f32[32,32,128]{2,1,0:T(8,128)} %bitcast.10) | data formatting | bytes 1048576
  61.3 0.0 copy-done
  61.3 1.0 %copy.10 = f32[2,32,32,128]{3,2,1,0:T(8,128)} copy(f32[2,32,32,128]{3,2,1,0:T(8,128)S(1)} %bitcast.7) | data formatting | bytes 2097152
Async XLA Ops:
  59.3 2.0 %copy-start = (f32[2,1024,128]{2,1,0:T(8,128)S(1)}, f32[2,1024,128]{2,1,0:T(8,128)}, u32[]{:S(2)}) copy-start(f32[2,1024,128]{2,1,0:T(8,128)} %get-tuple-element.5) | copy-start | bytes 3145732

commit v4 on v3

--- a/solution.py
+++ b/solution.py
@@ -60,7 +60,7 @@
         return v if isinstance(n, int) and n == 0 else pltpu.roll(v, n, 1)
 
     def back(x):
-        return lax.rem(2 * LANES - 2 * x - 1, LANES)
+        return -2 * x - 1 if isinstance(x, int) else lax.rem(2 * LANES - 2 * x - 1, LANES)
 
     low = lanes(1) < HALF
     odd = lanes(1) % 2 == 1
@@ -83,7 +83,7 @@
     def fold(v):
         return jnp.sum(v.reshape(groups, 8, LANES), axis=0)
 
-    def sweep(body, pack=0, sums=0, unroll=UNROLL, early=None):
+    def sweep(body, pack=0, sums=0, unroll=UNROLL, early=None, after=None):
         zero = jnp.zeros((cy, LANES), jnp.float32)
 
         def step(x, carry):
@@ -98,7 +98,8 @@
             return lax.fori_loop(0, cx, step, start, unroll=unroll)
         for x in (*range(GHOST), *range(cx - GHOST, cx)):
             start = step(x, start)
-        send_x(early)
+        send_x(early, start[0])
+        far(after)
         return lax.fori_loop(GHOST, cx - GHOST, step, start, unroll=7)
 
     def copies(e):
@@ -111,6 +112,10 @@
                 src_ref=src, dst_ref=dst, send_sem=send_sem.at[e, n], recv_sem=recv_sem.at[e, n],
                 device_id=device_at(offset), device_id_type=MESH))
 
+        corners = list(itertools.product((-1, 1), repeat=2)) if deep else []
+        for n, (a, b) in enumerate(corners):
+            add((a, 0, b), xzsend.at[e, n], xzrecv.at[e, n])
+            add((a, b, 0), xysend.at[e, n], xyrecv.at[e, n])
         for k in range(2):
             for j in range(GHOST) if deep else (0,):
                 add((-1, 0, 0), ext.at[e, pl.ds(at(k, GHOST + j, PAD), cy)],
@@ -118,29 +123,40 @@
                 add((1, 0, 0), ext.at[e, pl.ds(at(k, GHOST + cx - 1 - j, PAD), cy)],
                     ext.at[e, pl.ds(at(k, GHOST - 1 - j, PAD), cy)])
         near = len(out)
+        for a, b in corners:
+            tile = slice(0, 8) if a < 0 else slice(cy - 8, cy)
+            into = slice(PAD + cy, 2 * PAD + cy) if a < 0 else slice(0, PAD)
+            add((0, a, b), zsend.at[e, (b + 1) // 2, tile], zrecv.at[e, (b + 1) // 2, into])
         add((0, 0, -1), zsend.at[e, 0], zrecv.at[e, 0, PAD:PAD + cy])
         add((0, 0, 1), zsend.at[e, 1], zrecv.at[e, 1, PAD:PAD + cy])
         planes = slice(0, GHOST if deep else 1)
         for side in range(2):
             add((0, 2 * side - 1, 0), ysend.at[e, side, planes], yrecv.at[e, side, planes])
-        if deep:
+        return out[:near], out[near:]
+
+    def both_sides(faces):
+        return jnp.where(odd, faces[0], roll(faces[1], -1)), jnp.where(odd, roll(faces[1], 1), faces[0])
+
+    def send_x(e, faces=None):
+        if e in DEEP:
+            sides = both_sides(faces)
             for n, (a, b) in enumerate(itertools.product((-1, 1), repeat=2)):
-                add((a, b, 0), xysend.at[e, n], xyrecv.at[e, n])
-                add((a, 0, b), xzsend.at[e, n], xzrecv.at[e, n])
-                tile = slice(0, 8) if a < 0 else slice(cy - 8, cy)
-                into = slice(PAD + cy, 2 * PAD + cy) if a < 0 else slice(0, PAD)
-                add((0, a, b), zsend.at[e, (b + 1) // 2, tile], zrecv.at[e, (b + 1) // 2, into])
-        return out[:near], out[near:]
-
-    def send_x(e):
+                for k in range(2):
+                    row = at(k, GHOST + (cx - 1 if a > 0 else 0), PAD + (cy - 1 if b > 0 else 0))
+                    xysend[e, n, k:k + 1] = ext[e, row:row + 1, :]
+                lane = (2 * (cx - 1) if a > 0 else 0) + (0 if b > 0 else 1)
+                packed = jnp.zeros((8, LANES), jnp.float32)
+                for g in range(groups):
+                    part = roll(sides[(b + 1) // 2][8 * g:8 * g + 8], 2 * g)
+                    packed = jnp.where(lanes(8) % HALF == (lane + 2 * g) % HALF, part, packed)
+                xzsend[e, n] = packed
         for copy in copies(e)[0]:
             copy.start()
 
     def send(e, faces):
         zown[e] = faces[0]
         if e in DEEP:
-            zsend[e, 0] = jnp.where(odd, faces[0], roll(faces[1], -1))
-            zsend[e, 1] = jnp.where(odd, roll(faces[1], 1), faces[0])
+            zsend[e, 0], zsend[e, 1] = both_sides(faces)
         else:
             zsend[e, 0] = faces[0]
             zsend[e, 1] = faces[0]
@@ -149,54 +165,52 @@
                 y = cy - 1 - plane if side else plane
                 for k in range(2):
                     ysend[e, side, plane, k * cx:(k + 1) * cx] = ext[e, pl.ds(at(k, GHOST, PAD + y), cx, stride=pitch), :]
-        if e in DEEP:
-            for n, (a, b) in enumerate(itertools.product((-1, 1), repeat=2)):
-                for k in range(2):
-                    row = at(k, GHOST + (cx - 1 if a > 0 else 0), PAD + (cy - 1 if b > 0 else 0))
-                    xysend[e, n, k:k + 1] = ext[e, row:row + 1, :]
-                lane = (2 * (cx - 1) if a > 0 else 0) + (0 if b > 0 else 1)
-                packed = jnp.zeros((8, LANES), jnp.float32)
-                for g in range(groups):
-                    part = roll(zsend[e, (b + 1) // 2, 8 * g:8 * g + 8], 2 * g)
-                    packed = jnp.where(lanes(8) % HALF == (lane + 2 * g) % HALF, part, packed)
-                xzsend[e, n] = packed
         for copy in copies(e)[1]:
             copy.start()
 
     def arrive(e):
-        for copy in sum(copies(e), []):
+        faces, others = copies(e)
+        planes = GHOST if e in DEEP else 1
+        for copy in faces + others[-2:]:
             copy.wait()
         for side in range(2):
-            for plane in range(GHOST if e in DEEP else 1):
+            for plane in range(planes):
                 for k in range(2):
                     row = at(k, GHOST, PAD - 1 - plane if side else pitch + plane)
                     ext[e, pl.ds(row, cx, stride=pitch), :] = yrecv[e, side, plane, k * cx:(k + 1) * cx]
+        if e in DEEP:
+            side_x = [[None, None], [None, None]]
+            for n, (a, b) in enumerate(itertools.product((-1, 1), repeat=2)):
+                for k in range(2):
+                    row = at(k, GHOST - 1 if a > 0 else GHOST + cx, PAD - 1 if b > 0 else pitch)
+                    ext[e, row:row + 1, :] = xyrecv[e, n, k:k + 1]
+                lane = (2 * (cx - 1) if a > 0 else 0) + (0 if b > 0 else 1)
+                shift = -(lane + HALF) if b > 0 else HALF - 1 - lane
+                side_x[0 if a > 0 else 1][0 if b > 0 else 1] = [
+                    roll(xzrecv[e, n], shift - 2 * g) for g in range(groups)]
+            for side in range(2):
+                for g in range(groups):
+                    xe[side, 8 * g:8 * g + 8] = jnp.where(first, side_x[side][0][g], side_x[side][1][g])
+            pos = lanes(1) % HALF
+            left_x, right_x = roll(xe[0], 1), roll(xe[1], 2 * cx - 1)
+            uz[...] = zown[e] + jnp.where(pos < 2, left_x, 0.0) + jnp.where((pos >= 2 * cx - 2) & (pos < 2 * cx), right_x, 0.0)
+        for copy in others[:-2]:
+            copy.wait()
         if e not in DEEP:
             left, right = zrecv[e, 1, PAD:PAD + cy], zrecv[e, 0, PAD:PAD + cy]
             cp[PAD:] = jnp.where(odd, roll(left, HALF + 1), roll(right, HALF - 1))
             return
         left, right = zrecv[e, 1], zrecv[e, 0]
-        ck[...] = jnp.where(odd, roll(left, HALF + 1), roll(right, HALF - 1))
-        side_x = [[None, None], [None, None]]
-        for n, (a, b) in enumerate(itertools.product((-1, 1), repeat=2)):
-            for k in range(2):
-                row = at(k, GHOST - 1 if a > 0 else GHOST + cx, PAD - 1 if b > 0 else pitch)
-                ext[e, row:row + 1, :] = xyrecv[e, n, k:k + 1]
-            lane = (2 * (cx - 1) if a > 0 else 0) + (0 if b > 0 else 1)
-            shift = -(lane + HALF) if b > 0 else HALF - 1 - lane
-            side_x[0 if a > 0 else 1][0 if b > 0 else 1] = [
-                roll(xzrecv[e, n], shift - 2 * g) for g in range(groups)]
-        for side in range(2):
-            for g in range(groups):
-                xe[side, 8 * g:8 * g + 8] = jnp.where(first, side_x[side][0][g], side_x[side][1][g])
+        both = jnp.where(odd, roll(left, HALF + 1), roll(right, HALF - 1))
+        ck[...] = both
+        beyond = roll(jnp.where(odd, left[PAD:PAD + cy], right[PAD:PAD + cy]), HALF)
+        mid = both[PAD:PAD + cy]
+        cp[PAD:] = mid
         top = lax.broadcasted_iota(jnp.int32, (PAD, LANES), 0) == 0
-        cp[0:PAD] = jnp.where(top, roll(ck[PAD + cy:], 2), ck[0:PAD])
-        mid = ck[PAD:PAD + cy]
-        cp[PAD:] = mid
-        around = jnp.where(odd, roll(left[PAD:PAD + cy], HALF), roll(right[PAD:PAD + cy], HALF)) + zown[e]
-        pos = lanes(1) % HALF
-        around = around + jnp.where(pos < 2, roll(xe[0], 1), roll(mid, 2))
-        around = around + jnp.where((pos >= 2 * cx - 2) & (pos < 2 * cx), roll(xe[1], 2 * cx - 1), roll(mid, -2))
+        cp[0:PAD] = jnp.where(top, roll(both[PAD + cy:], 2), both[0:PAD])
+        around = uz[...] + beyond
+        around = around + jnp.where(pos < 2, 0.0, roll(mid, 2))
+        around = around + jnp.where((pos >= 2 * cx - 2) & (pos < 2 * cx), 0.0, roll(mid, -2))
         around = around + (ck[PAD - 1:PAD + cy - 1] + ck[PAD + 1:PAD + cy + 1])
         uz[...] = kz[...] * mid - around
 
@@ -214,21 +228,25 @@
             out.append(ext[KAP, pl.ds(b, rows), :] * center[k] - (around + beside[k]))
         return out
 
-    def wide(e):
-        src, dst = ext.at[e], uext.at[e]
-
-        def put(base, rows, edge):
-            for k, v in enumerate(apply(src, base, rows, edge)):
-                dst[pl.ds(pl.multiple_of(base + k * block, 8), rows), :] = v
-
-        put(at(0, GHOST - 1, PAD), cy, xe[0])
-
+    def put(e, base, rows, edge):
+        for k, v in enumerate(apply(ext.at[e], base, rows, edge)):
+            uext[e, pl.ds(pl.multiple_of(base + k * block, 8), rows), :] = v
+
+    def wide(e, x):
+        put(e, at(0, x + GHOST), pitch, roll(cp[...], back(x)))
+
+    def near(e):
+        put(e, at(0, GHOST - 1, PAD), cy, xe[0])
+        for x in (*range(GHOST + 1), *range(cx - GHOST - 1, cx)):
+            wide(e, x)
+        put(e, at(0, GHOST + cx, PAD), cy, xe[1])
+        put(e, at(0, GHOST + cx), PAD, roll(cp[0:PAD], -2 * cx - 1))
+
+    def far(e):
         def step(x, carry):
-            put(at(0, x + GHOST), pitch, roll(cp[...], back(x)))
+            wide(e, x)
             return carry
-        lax.fori_loop(0, cx, step, 0, unroll=UNROLL)
-        put(at(0, GHOST + cx, PAD), cy, xe[1])
-        put(at(0, GHOST + cx), PAD, roll(cp[0:PAD], -2 * cx - 1))
+        lax.fori_loop(GHOST + 1, cx - GHOST - 1, step, 0, unroll=13)
 
     def again(e, x):
         return apply(uext.at[e], at(0, x + GHOST, PAD), cy, roll(uz[...], back(x)))
@@ -265,8 +283,8 @@
         return jnp.take_along_axis(v, index, axis=1)
 
     lane = lanes(cy)
-    apart = 2 * (lane % HALF) + lane // HALF
-    together = lane // 2 + HALF * (lane % 2)
+    apart = [2 * (lane % HALF) + (lane // HALF if s == 0 else 1 - lane // HALF) for s in range(sets)]
+    together = [lane // 2 + HALF * (lane % 2 if s == 0 else 1 - lane % 2) for s in range(sets)]
 
     def permute(ref, index, rows):
         def step(m, carry):
@@ -277,19 +295,17 @@
 
     def split(ref, x):
         a, b = ref[0, plain(x), :], ref[1, plain(x), :]
-        return jnp.where(low, a, roll(b, HALF)), jnp.where(low, roll(a, HALF), b)
+        return jnp.where(low, a, b), roll(jnp.where(low, b, a), HALF)
 
     def join(even_z, odd_z):
-        return jnp.where(low, even_z, roll(odd_z, HALF)), jnp.where(low, roll(even_z, HALF), odd_z)
+        turned = roll(odd_z, HALF)
+        return jnp.where(low, even_z, turned), jnp.where(low, turned, even_z)
 
     def keep(e, x, pair):
         for k in range(2):
             ext[e, inner(k, x), :] = pair[k]
 
     def load(e, ref):
-        for s in range(sets):
-            permute(ref.at[s], apart, lines)
-
         def body(x):
             pair = split(ref, x)
             keep(e, x, pair)
@@ -335,40 +351,39 @@
         lax.fori_loop(0, 1, step, 0)
 
     loads[0].wait()
+    for s in range(sets):
+        permute(start_ref.at[s], apart[s], lines)
     faces_start = load(X0, start_ref)
     loads[3].wait()
-    permute(lr_ref, apart, lines)
+    permute(lr_ref, apart[0], lines)
     faces_kap = sweep(load_kap, 1)[0]
     pl.semaphore_wait(barrier, total - 1)
-    send_x(X0)
+    send_x(X0, faces_start)
     send(X0, faces_start)
     send_x(KAP)
     send(KAP, faces_kap)
     loads[4].wait()
-    faces_state = load(STATE, state_ref)
-    send_x(STATE)
-    send(STATE, faces_state)
+    for s in range(sets):
+        permute(state_ref.at[s], apart[s], lines)
     loads[1].wait()
     loads[2].wait()
     observe(0)
     observe(1)
 
-    def mix(n, x):
-        a, b = raw[0, n, plain(x), :], raw[1, n, plain(x), :]
-        return jnp.where(low, a, b), roll(jnp.where(low, b, a), HALF)
-
     def right_pass(x):
-        count, amount = mix(0, x), mix(1, x)
-        for k in range(2):
-            weight[dense(k, x), :] = count[k]
-            rhs[dense(k, x), :] = amount[k] - count[k] * (ext[STATE, inner(k, x), :] + ext[X0, inner(k, x), :])
+        here = plain(x)
+        counts = [raw[s, 0, here, :] for s in range(sets)]
+        right = [raw[s, 1, here, :] - counts[s] * (state_ref[s, here, :] + start_ref[s, here, :]) for s in range(sets)]
+        for ref, (a, b) in ((weight, counts), (rhs, right)):
+            ref[dense(0, x), :] = jnp.where(low, a, b)
+            ref[dense(1, x), :] = roll(jnp.where(low, b, a), HALF)
         return (None, None), ()
 
     sweep(right_pass)
     arrive(KAP)
     kz[...] = cp[PAD:]
     arrive(X0)
-    wide(X0)
+    near(X0)
 
     def residual_pass(x):
         out = again(X0, x)
@@ -376,20 +391,14 @@
         keep(R0, x, pair)
         return pair, ()
 
-    send(R0, sweep(residual_pass, 2, early=R0)[0])
-
-    arrive(STATE)
-
-    def state_pass(x):
-        out = once(STATE, x)
-        for k in range(2):
-            ast[dense(k, x), :] = out[k]
-        return (None, None), ()
-
-    sweep(state_pass)
+    send(R0, sweep(residual_pass, 2, early=R0, after=X0)[0])
+
+    faces = load(STATE, state_ref)
+    send_x(STATE)
+    send(STATE, faces)
 
     arrive(R0)
-    wide(R0)
+    near(R0)
 
     def image_pass(x):
         out = again(R0, x)
@@ -398,22 +407,24 @@
         keep(W0, x, pair)
         return pair, (now[0] * now[0] + now[1] * now[1], now[0] * pair[0] + now[1] * pair[1])
 
-    faces, gathered = sweep(image_pass, 2, 2, early=W0)
+    faces, gathered = sweep(image_pass, 2, 2, early=W0, after=R0)
+    reduce_start(0, gathered)
     send(W0, faces)
-    reduce_start(0, gathered)
+
+    arrive(STATE)
+
+    def state_pass(x):
+        out = once(STATE, x)
+        for k in range(2):
+            ast[dense(k, x), :] = out[k]
+        return (None, None), ()
+
+    sweep(state_pass)
 
     norms, steps, ratios = [], [], []
     for k, e in enumerate((W0, W1)):
         arrive(e)
-        wide(e)
-
-        def next_image(x, e=e):
-            out = again(e, x)
-            for p in range(2):
-                q[dense(p, x), :] = out[p] + weight[dense(p, x), :] * ext[e, inner(p, x), :]
-            return (None, None), ()
-
-        sweep(next_image)
+        near(e)
         norm, product = reduce_end(k)
         if k == 0:
             ratio, step_size = None, norm / product
@@ -425,10 +436,11 @@
         ratios.append(ratio)
 
         def update(x, k=k, e=e, ratio=ratio, step_size=step_size):
-            pair, terms = [], []
+            pair, terms, out = [], [], again(e, x)
             for p in range(2):
                 here, there = dense(p, x), inner(p, x)
-                image, vec = q[here, :], ext[e, there, :]
+                vec = ext[e, there, :]
+                image = out[p] + weight[here, :] * vec
                 if k == 0:
                     z[here, :] = image
                     follow, now = vec, ext[R0, there, :]
@@ -444,9 +456,9 @@
                 terms.append((now * now, now * vec))
             return pair, (terms[0][0] + terms[1][0], terms[0][1] + terms[1][1])
 
-        faces, gathered = sweep(update, 2 if e + 1 in DEEP else 1, 2, early=e + 1)
+        faces, gathered = sweep(update, 2 if e + 1 in DEEP else 1, 2, early=e + 1, after=e)
+        reduce_start(k + 1, gathered)
         send(e + 1, faces)
-        reduce_start(k + 1, gathered)
 
         def trail(x, k=k, ratio=ratio, step_size=step_size):
             for p in range(2):
@@ -524,20 +536,17 @@
             for s, v in enumerate(join(*pair)):
                 raw[s, n, here, :] = v
         parts = [join(grads[0][n], grads[1][n]) for n in range(3)]
-        grad_ref[here, :] = scale * (parts[0][0] + parts[0][1])
-        for s in range(sets):
-            gr[s, here, :] = scale * parts[1][s]
-            gd[s, here, :] = scale * parts[2][s]
+        grad_ref[here, :] = scale * (parts[0][0] + roll(parts[0][1], HALF))
+        for s, factor in enumerate((scale, roll(scale, HALF))):
+            gr[s, here, :] = factor * parts[1][s]
+            gd[s, here, :] = factor * parts[2][s]
         return (None, None), ()
 
     sweep(prepare, unroll=4)
     for s in range(sets):
-        permute(adj_ref.at[s], together, lines)
-        for n in range(2):
-            permute(raw.at[s, n], together, lines)
-        permute(gr.at[s], together, lines)
-        permute(gd.at[s], together, lines)
-    permute(grad_ref, together, lines)
+        for ref in (adj_ref.at[s], raw.at[s, 0], raw.at[s, 1], gr.at[s], gd.at[s]):
+            permute(ref, together[s], lines)
+    permute(grad_ref, together[0], lines)
     last_norm, last_product = reduce_end(3)
     last_ratio = last_norm / norm
     last_step = last_norm / (last_product - last_ratio * last_norm / step_size)

time: 62.4 us -> 59 us (0.946)
  Pallas kernels: 58.7 us -> 55.3 us
    pallas_call x1, Pallas kernels: 58.7 us -> 55.3 us  [on_device(): pl.pallas_call(functools.partial(kernel, sizes, (sets, cx, cy, cz, nobs))...]
where the time goes in v4:
time: 59 us; the launch traced here: 58.9 us
  Pallas kernels  55.3 us (94%)
  local copies, waits for them, and re-layouts  2.93 us (5%)
  between operations  0.65 us (1%)
    pallas_call x1, Pallas kernels, on_device(): pl.pallas_call(functools.partial(kernel, sizes, (sets, cx, cy, cz, nobs))...  55.3 us
    unnamed x4, local copies, waits for them, and re-layouts  2.93 us

profile of v4, /device:TPU:0, one launch (start us, length us, event | category | flops | bytes accessed | tf_op | source)
XLA Modules:
  0.0 58.9 jit_solution(11287329544679196489)
XLA Ops:
  0.6 55.3 %shard_map.68 = (f32[1024,128]{1,0:T(8,128)}, f32[2,1024,128]{2,1,0:T(8,128)}) custom-call(f32[1024,128]{1,0:T(8,128)} %bitcast.11, f32[2,1024,128]{2,1,0:T(8,128)} %bitcast.8, f32[2,1024,128]{2,1,0:T(8,128)} %bitcast.9, s32[2,1,4096]{2,1,0:T(1,128)} %bitcast.12, f32[2,1,4096]{2,1,0:T(1,128)} %bitcast.13), custom_call_target="tpu_custom_call" | custom-call | tf_op jit(solution)/shard_map/pallas_call | solution.py:578
  55.9 0.0 copy-start
  55.9 2.0 %copy.9 = f32[32,32,128]{2,1,0:T(8,128)} copy(f32[32,32,128]{2,1,0:T(8,128)} %bitcast.10) | data formatting | bytes 1048576
  57.9 0.0 copy-done
  57.9 1.0 %copy.10 = f32[2,32,32,128]{3,2,1,0:T(8,128)} copy(f32[2,32,32,128]{3,2,1,0:T(8,128)S(1)} %bitcast.7) | data formatting | bytes 2097152
Async XLA Ops:
  55.9 2.0 %copy-start = (f32[2,1024,128]{2,1,0:T(8,128)S(1)}, f32[2,1024,128]{2,1,0:T(8,128)}, u32[]{:S(2)}) copy-start(f32[2,1024,128]{2,1,0:T(8,128)} %get-tuple-element.5) | copy-start | bytes 3145732

commit v5 on v4

--- a/solution.py
+++ b/solution.py
@@ -16,6 +16,7 @@
 AXES = ("gx", "gy", "gz")
 MESH = pl.DeviceIdType.MESH
 UNROLL = 8
+CHUNKS = 4
 X0, R0, W0, W1, W2, STATE, KAP, FIELDS = range(8)
 DEEP = (X0, R0, W0, W1)
 COPIES = 24
@@ -24,10 +25,10 @@
 
 
 def kernel(
-    sizes, dims, lr_hbm, state_hbm, start_hbm, idx_hbm, val_hbm, grad_ref, adj_ref,
-    lr_ref, state_ref, start_ref, idx_ref, val_ref, ext, uext, ysend, yrecv, zsend, zrecv, zown, xysend, xyrecv, xzsend, xzrecv,
+    sizes, dims, lr_hbm, state_hbm, start_hbm, idx_hbm, val_hbm, grad_hbm, adj_hbm,
+    grad_ref, adj_ref, lr_ref, state_ref, start_ref, idx_ref, val_ref, ext, uext, ysend, yrecv, zsend, zrecv, zown, xysend, xyrecv, xzsend, xzrecv,
     ck, cp, xe, uz, kz, kap, cols, raw, weight, rhs, z, s_buf, r, ar, q, ast, ad, xs, axs,
-    gr, gd, red_out, red, send_sem, recv_sem, red_send, red_recv, load_sem,
+    gr, gd, red_out, red, send_sem, recv_sem, red_send, red_recv, load_sem, store_sem,
 ):
     sets, cx, cy, cz, nobs = dims
     pitch = cy + PAD
@@ -562,7 +563,36 @@
             grad = grad + (one[s] * gr[s, here, :] + two[s] * gd[s, here, :])
         grad_ref[here, :] = grad
         return carry
-    lax.fori_loop(0, cx, finish, 0, unroll=UNROLL)
+    stores = []
+    for c in range(CHUNKS):
+        lax.fori_loop(c * cx // CHUNKS, (c + 1) * cx // CHUNKS, finish, 0, unroll=True)
+        part = slice(c * lines // CHUNKS, (c + 1) * lines // CHUNKS)
+        targets = [(grad_ref.at[part], grad_hbm.at[part])]
+        targets += [(adj_ref.at[s, part], adj_hbm.at[s, part]) for s in range(sets)]
+        for n, (src, dst) in enumerate(targets):
+            stores.append(pltpu.make_async_copy(src, dst, store_sem.at[c, n]))
+            stores[-1].start()
+    for copy in stores:
+        copy.wait()
+
+
+def hand_over(grad_in, adj_in, grad_out, adj_out, buf, in_sem, out_sem):
+    sets, rows, _ = adj_in.shape
+    half = rows // 2
+    pairs = []
+    for h in range(2):
+        part = slice(h * half, (h + 1) * half)
+        pairs.append((grad_in.at[part], grad_out.at[part]))
+        pairs += [(adj_in.at[s, part], adj_out.at[s, part]) for s in range(sets)]
+    loads = [pltpu.make_async_copy(a, buf.at[n], in_sem.at[n]) for n, (a, b) in enumerate(pairs)]
+    stores = [pltpu.make_async_copy(buf.at[n], b, out_sem.at[n]) for n, (a, b) in enumerate(pairs)]
+    for copy in loads:
+        copy.start()
+    for load, store in zip(loads, stores):
+        load.wait()
+        store.start()
+    for copy in stores:
+        copy.wait()
 
 
 def on_device(sizes, log_range, state, adjoint_start, obs_index, obs_value):
@@ -574,16 +604,18 @@
     f32 = jnp.float32
     field = pltpu.VMEM((2 * rows, LANES), f32)
     natural = pltpu.VMEM((sets, rows, cz), f32)
-    vmem = pl.BlockSpec(memory_space=pltpu.VMEM)
+    hbm = pl.BlockSpec(memory_space=pltpu.HBM)
     gradient, adjoint = pl.pallas_call(
         functools.partial(kernel, sizes, (sets, cx, cy, cz, nobs)),
         out_shape=(
             jax.ShapeDtypeStruct((rows, cz), jnp.float32),
             jax.ShapeDtypeStruct((sets, rows, cz), jnp.float32),
         ),
-        in_specs=[pl.BlockSpec(memory_space=pltpu.HBM)] * 5,
-        out_specs=(vmem, vmem),
+        in_specs=[hbm] * 5,
+        out_specs=(hbm, hbm),
         scratch_shapes=[
+            pltpu.VMEM((rows, cz), f32),
+            natural,
             pltpu.VMEM((rows, cz), f32),
             natural,
             natural,
@@ -617,6 +649,7 @@
             pltpu.SemaphoreType.DMA((ITERS,)),
             pltpu.SemaphoreType.DMA((ITERS,)),
             pltpu.SemaphoreType.DMA((5,)),
+            pltpu.SemaphoreType.DMA((CHUNKS, 1 + sets)),
         ],
         compiler_params=pltpu.CompilerParams(
             collective_id=0, has_side_effects=True, vmem_limit_bytes=63 * 1024 * 1024
@@ -628,6 +661,20 @@
         obs_index.reshape(sets, 1, nobs),
         obs_value.reshape(sets, 1, nobs),
     )
+    gradient, adjoint = pl.pallas_call(
+        hand_over,
+        out_shape=(
+            jax.ShapeDtypeStruct((rows, cz), jnp.float32),
+            jax.ShapeDtypeStruct((sets, rows, cz), jnp.float32),
+        ),
+        in_specs=[hbm] * 2,
+        out_specs=(hbm, hbm),
+        scratch_shapes=[
+            pltpu.VMEM((2 + 2 * sets, rows // 2, cz), f32),
+            pltpu.SemaphoreType.DMA((2 + 2 * sets,)),
+            pltpu.SemaphoreType.DMA((2 + 2 * sets,)),
+        ],
+    )(gradient, adjoint)
     return gradient.reshape(cx, cy, cz), adjoint.reshape(sets, cx, cy, cz)
 
 

time: 59 us -> 58.3 us (0.988)
  local copies, waits for them, and re-layouts: 2.93 us -> 0 us
  Pallas kernels: 55.3 us -> 57.3 us
    unnamed x4 -> x0, local copies, waits for them, and re-layouts: 2.93 us -> none
    pallas_call x0 -> x1, Pallas kernels: none -> 2.19 us  [on_device(): pl.pallas_call(hand_over, out_shape=(jax.ShapeDtypeStruct((rows, cz), jnp...]
where the time goes in v5:
time: 58.3 us; the launch traced here: 58.1 us
  Pallas kernels  57.3 us (98%)
  between operations  0.8 us (1%)
    pallas_call x1, Pallas kernels, on_device(): pl.pallas_call(functools.partial(kernel, sizes, (sets, cx, cy, cz, nobs))...  55.1 us
    pallas_call x1, Pallas kernels, on_device(): pl.pallas_call(hand_over, out_shape=(jax.ShapeDtypeStruct((rows, cz), jnp...  2.19 us

profile of v5, /device:TPU:0, one launch (start us, length us, event | category | flops | bytes accessed | tf_op | source)
XLA Modules:
  0.0 58.1 jit_solution(2042882912631573044)
XLA Ops:
  0.6 55.1 %shard_map.68 = (f32[1024,128]{1,0:T(8,128)}, f32[2,1024,128]{2,1,0:T(8,128)}) custom-call(f32[1024,128]{1,0:T(8,128)} %bitcast.9, f32[2,1024,128]{2,1,0:T(8,128)} %bitcast.7, f32[2,1024,128]{2,1,0:T(8,128)} %bitcast.8, s32[2,1,4096]{2,1,0:T(1,128)} %bitcast.10, f32[2,1,4096]{2,1,0:T(1,128)} %bitcast.11), custom_call_target="tpu_custom_call" | custom-call | tf_op jit(solution)/shard_map/pallas_call | solution.py:608
  55.7 2.2 %shard_map.69 = (f32[1024,128]{1,0:T(8,128)}, f32[2,1024,128]{2,1,0:T(8,128)}) custom-call(f32[1024,128]{1,0:T(8,128)} %get-tuple-element.6.grad_in, f32[2,1024,128]{2,1,0:T(8,128)} %get-tuple-element.7.adj_in), custom_call_target="tpu_custom_call" | custom-call | tf_op jit(solution)/shard_map/pallas_call | solution.py:664
